TPU v7x, 16 devices: a whole 2x2x2 slice. The times are simulated.
16 devices in a mesh: dp: 4 (over z, y), tp: 4 (over x, core).
Axes of the slice: x: 2, y: 2, z: 2, core: 2. Of those that a mesh axis runs over, the one named last changes fastest.
Arguments:
- hidden_in: bfloat16 [8, 2048, 1280], P('dp', 'tp'), parts along dimension 0
- norms: float32 [2, 4, 1280], replicated
- w_qkv: bfloat16 [2, 1280, 3, 20, 64], P(None, None, None, 'tp')
- w_out: bfloat16 [2, 20, 64, 1280], P(None, 'tp')
- b_out: float32 [2, 1280], replicated
- w_up: bfloat16 [2, 1280, 5120], P(None, None, 'tp')
- b_up: float32 [2, 5120], P(None, 'tp')
- w_down: bfloat16 [2, 5120, 1280], P(None, 'tp')
- b_down: float32 [2, 1280], replicated
Outputs:
- output: bfloat16 [8, 2048, 1280], P('dp', 'tp'), parts along dimension 0
There are 4 independent parts. A program takes and returns all parts, laid end to end along the dimension named above; an argument that names none is the same for every part.
All inputs are finite; a program needn't handle non-finite values.
Results may differ from a plain program's by a relative error of at most 0.0124455.
Values are sent between devices in bfloat16 or wider.
A program may use at most 1 GiB of HBM per device.

v0:
```python
import jax
import jax.numpy as jnp
from jax import lax
from jax.sharding import PartitionSpec as P

LN_EPS = 1e-5


def layer_norm(rows, gain, shift):
    row_mean = jnp.mean(rows, axis=-1, keepdims=True)
    centred = rows - row_mean
    row_var = jnp.mean(centred * centred, axis=-1, keepdims=True)
    return (centred * lax.rsqrt(row_var + LN_EPS) * gain + shift).astype(jnp.bfloat16)


def attention(qkv_rows, head_dim):
    scores = jnp.einsum('bqhe,bkhe->bhqk', qkv_rows[:, :, 0], qkv_rows[:, :, 1], preferred_element_type=jnp.float32) * head_dim ** -0.5
    attn_prob = jax.nn.softmax(scores, axis=-1).astype(jnp.bfloat16)
    return jnp.einsum('bhqk,bkhe->bqhe', attn_prob, qkv_rows[:, :, 2], preferred_element_type=jnp.float32).astype(jnp.bfloat16)


def reduce_rows(partial, group_size):
    batch_loc, seq_len, width = partial.shape
    received = lax.all_to_all(partial.astype(jnp.bfloat16), 'tp', 1, 0, tiled=True)
    received = received.reshape(group_size, batch_loc, seq_len // group_size, width)
    return jnp.sum(received.astype(jnp.float32), axis=0)


def solution(mesh):
    group_size = mesh.shape['tp']

    def local_layers(hidden_in, norms, w_qkv, w_out, b_out, w_up, b_up, w_down, b_down):
        head_dim = w_qkv.shape[-1]
        residual = hidden_in.astype(jnp.float32)
        for layer_idx in range(w_qkv.shape[0]):
            normed = layer_norm(residual, norms[layer_idx, 0], norms[layer_idx, 1])
            full_rows = lax.all_gather(normed, 'tp', axis=1, tiled=True)
            qkv_rows = jnp.einsum('bsd,dthe->bsthe', full_rows, w_qkv[layer_idx], preferred_element_type=jnp.float32).astype(jnp.bfloat16)
            attn_rows = attention(qkv_rows, head_dim)
            partial = jnp.einsum('bshe,hed->bsd', attn_rows, w_out[layer_idx], preferred_element_type=jnp.float32)
            residual = residual + reduce_rows(partial, group_size) + b_out[layer_idx]
            normed2 = layer_norm(residual, norms[layer_idx, 2], norms[layer_idx, 3])
            full_rows2 = lax.all_gather(normed2, 'tp', axis=1, tiled=True)
            hidden = jnp.einsum('bsd,df->bsf', full_rows2, w_up[layer_idx], preferred_element_type=jnp.float32) + b_up[layer_idx]
            gelu_out = jax.nn.gelu(hidden, approximate=True).astype(jnp.bfloat16)
            partial2 = jnp.einsum('bsf,fd->bsd', gelu_out, w_down[layer_idx], preferred_element_type=jnp.float32)
            residual = residual + reduce_rows(partial2, group_size) + b_down[layer_idx]
        return residual.astype(jnp.bfloat16)

    in_specs = (P('dp', 'tp', None), P(), P(None, None, None, 'tp', None), P(None, 'tp', None, None), P(), P(None, None, 'tp'), P(None, 'tp'), P(None, 'tp', None), P())
    return jax.shard_map(local_layers, mesh=mesh, in_specs=in_specs, out_specs=P('dp', 'tp', None), check_vma=False)
```

profile of v0, /device:TPU:0, one launch (start us, length us, event | category | flops | bytes accessed | tf_op | source)
XLA Modules:
  0.0 1446.7 jit_solution(2924520629639662599)
XLA Ops:
  6.5 1.7 slice_reduce_fusion.3
  8.3 2.2 convert_reduce_fusion.4
  10.5 2.6 fusion.54
  13.0 2.5 fusion.57
  15.6 71.7 %all-gather.5.cloned.1.call-done = bf16[2,2048,1280]{2,1,0:T(8,128)(2,1)} async-done(((bf16[2,512,1280]{2,1,0:T(8,128)(2,1)}), bf16[2,2048,1280]{2,1,0:T(8,128)(2,1)}) %all-gather.5.cloned.1.call-update) | async-done | bytes 10485776 | tf_op jit(solution)/shard_map/all_gather | solution.py:37
  87.3 15.9 %fusion.63 = bf16[2,2048,3,5,64]{1,4,3,2,0:T(8,128)(2,1)} fusion(bf16[2,2048,1280]{2,1,0:T(8,128)(2,1)} %all-gather.5.cloned.1.call-done, bf16[2,1280,3,5,64]{1,4,3,2,0:T(8,128)(2,1)} %param.11), kind=kOutput, calls=%fused_computation.69 | convolution fusion | flops 10070261760 | bytes 20807680 | tf_op jit(solution)/shard_map/bsd,dthe->bsthe/dot_general | solution.py:38
  103.2 54.8 %fusion.134 = f32[2,5,2048]{2,1,0:T(8,128)S(1)} fusion(bf16[2,2048,3,5,64]{1,4,3,2,0:T(8,128)(2,1)} %fusion.63), kind=kOutput, calls=%fused_computation.138 | convolution fusion | flops 5494540288 | bytes 5324800 | tf_op jit(solution)/shard_map/sub | solution.py:18
  158.0 72.7 %fusion.93 = bf16[2,2048,5,64]{1,3,2,0:T(8,128)(2,1)} fusion(f32[2,5,2048]{2,1,0:T(8,128)S(1)} %fusion.134, bf16[2,2048,3,5,64]{1,4,3,2,0:T(8,128)(2,1)} %fusion.63), kind=kOutput, calls=%fused_computation.81 | convolution fusion | flops 10906523648 | bytes 10567680 | tf_op jit(solution)/shard_map/bhqk,bkhe->bqhe/dot_general | solution.py:19
  230.7 8.2 bitcast_convert_fusion.1
  239.0 74.2 %copy.15 = bf16[2,2048,1280]{2,0,1:T(2,128)(2,1)} copy(bf16[2,2048,1280]{2,1,0:T(8,128)(2,1)S(1)} %bitcast_convert_fusion.1) | data formatting | bytes 20971520 | tf_op jit(solution)/shard_map/convert_element_type | solution.py:24
  313.1 6.1 all-to-all-start
  319.3 0.6 slice_reduce_fusion.4
  319.9 114.6 %all-to-all-done = bf16[2,2048,1280]{2,0,1:T(2,128)(2,1)} async-done(((bf16[2,2048,1280]{2,0,1:T(2,128)(2,1)}), bf16[2,2048,1280]{2,0,1:T(2,128)(2,1)}, u32[]{:S(2)}, u32[]{:S(2)}) %all-to-all-start) | async-done | bytes 10485792 | tf_op jit(solution)/shard_map/all_to_all | solution.py:24
  434.5 19.2 %convert_reduce_fusion.3 = f32[2,512,1280]{2,0,1:T(2,128)S(1)} fusion(bf16[2,4,512,1280]{3,0,2,1:T(2,128)(2,1)} %bitcast.37), kind=kLoop, calls=%fused_computation.35 | loop fusion | flops 9175040 | bytes 15728640 | tf_op jit(solution)/shard_map/reduce_sum | solution.py:26
  453.7 0.8 fusion.129
  454.5 1.1 multiply_reduce_fusion.4
  455.7 0.4 copy-done
  456.1 2.4 add_convert_fusion.2
  458.5 0.6 slice_reduce_fusion.1
  459.1 68.3 %all-gather.7.cloned.1.call-done = bf16[2,2048,1280]{2,1,0:T(8,128)(2,1)} async-done(((bf16[2,512,1280]{2,1,0:T(8,128)(2,1)}), bf16[2,2048,1280]{2,1,0:T(8,128)(2,1)}) %all-gather.7.cloned.1.call-update) | async-done | bytes 10485776 | tf_op jit(solution)/shard_map/all_gather | solution.py:43
  527.4 38.7 %convolution_convert_fusion.1 = bf16[2,2048,1280]{2,1,0:T(8,128)(2,1)} fusion(bf16[2,2048,1280]{2,1,0:T(8,128)(2,1)} %all-gather.7.cloned.1.call-done, f32[1280]{0:T(1024)S(1)} %get-tuple-element.16, bf16[2,1280,1280]{2,1,0:T(8,128)(2,1)} %param.16, bf16[2,1280,1280]{2,1,0:T(8,128)(2,1)} %param.14), kind=kOutput, calls=%fused_computation.41 | convolution fusion | flops 26901217280 | bytes 27530240 | tf_op jit(solution)/shard_map/bsf,fd->bsd/dot_general | solution.py:46
  566.1 20.2 %copy.17 = bf16[2,2048,1280]{2,0,1:T(2,128)(2,1)} copy(bf16[2,2048,1280]{2,1,0:T(8,128)(2,1)} %convolution_convert_fusion.1) | data formatting | bytes 20971520 | tf_op jit(solution)/shard_map/convert_element_type | solution.py:24
  586.2 6.1 all-to-all-start.1
  592.5 0.6 slice_reduce_fusion
  593.1 114.6 %all-to-all-done.1 = bf16[2,2048,1280]{2,0,1:T(2,128)(2,1)} async-done(((bf16[2,2048,1280]{2,0,1:T(2,128)(2,1)}), bf16[2,2048,1280]{2,0,1:T(2,128)(2,1)}, u32[]{:S(2)}, u32[]{:S(2)}) %all-to-all-start.1) | async-done | bytes 10485792 | tf_op jit(solution)/shard_map/all_to_all | solution.py:24
  707.7 19.2 %convert_reduce_fusion.2 = f32[2,512,1280]{2,0,1:T(2,128)S(1)} fusion(bf16[2,4,512,1280]{3,0,2,1:T(2,128)(2,1)} %bitcast.38), kind=kLoop, calls=%fused_computation.34 | loop fusion | flops 9175040 | bytes 15728640 | tf_op jit(solution)/shard_map/reduce_sum | solution.py:26
  726.9 3.6 fusion.132
  730.5 0.7 multiply_reduce_fusion.3
  731.2 1.6 copy-done.3
  732.8 2.4 add_convert_fusion.1
  735.3 68.9 %all-gather.9.cloned.1.call-done = bf16[2,2048,1280]{2,1,0:T(8,128)(2,1)} async-done(((bf16[2,512,1280]{2,1,0:T(8,128)(2,1)}), bf16[2,2048,1280]{2,1,0:T(8,128)(2,1)}) %all-gather.9.cloned.1.call-update) | async-done | bytes 10485776 | tf_op jit(solution)/shard_map/all_gather | solution.py:37
  804.1 15.7 %fusion.66 = bf16[2,2048,3,5,64]{1,4,3,2,0:T(8,128)(2,1)} fusion(bf16[2,2048,1280]{2,1,0:T(8,128)(2,1)} %all-gather.9.cloned.1.call-done, bf16[2,1280,3,5,64]{1,4,3,2,0:T(8,128)(2,1)} %param.11), kind=kOutput, calls=%fused_computation.70 | convolution fusion | flops 10070261760 | bytes 20807680 | tf_op jit(solution)/shard_map/bsd,dthe->bsthe/dot_general | solution.py:38
  819.8 54.8 %fusion.135 = f32[2,5,2048]{2,1,0:T(8,128)S(1)} fusion(bf16[2,2048,3,5,64]{1,4,3,2,0:T(8,128)(2,1)} %fusion.66), kind=kOutput, calls=%fused_computation.139 | convolution fusion | flops 5494540288 | bytes 5324800 | tf_op jit(solution)/shard_map/sub | solution.py:18
  874.7 72.7 %fusion.98 = bf16[2,2048,5,64]{1,3,2,0:T(8,128)(2,1)} fusion(f32[2,5,2048]{2,1,0:T(8,128)S(1)} %fusion.135, bf16[2,2048,3,5,64]{1,4,3,2,0:T(8,128)(2,1)} %fusion.66), kind=kOutput, calls=%fused_computation.82 | convolution fusion | flops 10906523648 | bytes 10567680 | tf_op jit(solution)/shard_map/bhqk,bkhe->bqhe/dot_general | solution.py:19
  947.3 8.2 bitcast_convert_fusion
  955.6 74.9 %copy.20 = bf16[2,2048,1280]{2,0,1:T(2,128)(2,1)S(1)} copy(bf16[2,2048,1280]{2,1,0:T(8,128)(2,1)S(1)} %bitcast_convert_fusion) | data formatting | bytes 20971520 | tf_op jit(solution)/shard_map/convert_element_type | solution.py:24
  1030.5 118.5 %all_to_all.16 = bf16[2,2048,1280]{2,0,1:T(2,128)(2,1)S(1)} all-to-all(bf16[2,2048,1280]{2,0,1:T(2,128)(2,1)S(1)} %copy.20), channel_id=1, replica_groups=mesh['dp'=4,'tp'=4] {'tp'}, dimensions={1} | all-to-all | bytes 20971520 | tf_op jit(solution)/shard_map/all_to_all | solution.py:24
  1149.0 15.1 %convert_reduce_fusion.1 = f32[2,512,1280]{2,0,1:T(2,128)} fusion(bf16[2,4,512,1280]{3,0,2,1:T(2,128)(2,1)S(1)} %bitcast.159), kind=kLoop, calls=%fused_computation.33 | loop fusion | flops 9175040 | bytes 15728640 | tf_op jit(solution)/shard_map/reduce_sum | solution.py:26
  1164.1 3.2 fusion.130
  1167.3 0.7 multiply_reduce_fusion.2
  1168.0 1.6 copy-done.4
  1169.6 2.4 add_convert_fusion
  1172.0 68.9 %all-gather.11.cloned.1.call-done = bf16[2,2048,1280]{2,1,0:T(8,128)(2,1)} async-done(((bf16[2,512,1280]{2,1,0:T(8,128)(2,1)}), bf16[2,2048,1280]{2,1,0:T(8,128)(2,1)}) %all-gather.11.cloned.1.call-update) | async-done | bytes 10485776 | tf_op jit(solution)/shard_map/all_gather | solution.py:43
  1240.9 38.5 %convolution_convert_fusion = bf16[2,2048,1280]{2,1,0:T(8,128)(2,1)} fusion(bf16[2,2048,1280]{2,1,0:T(8,128)(2,1)} %all-gather.11.cloned.1.call-done, f32[1280]{0:T(1024)S(1)} %copy-done.16, bf16[2,1280,1280]{2,1,0:T(8,128)(2,1)} %param.16, bf16[2,1280,1280]{2,1,0:T(8,128)(2,1)} %param.14), kind=kOutput, calls=%fused_computation.40 | convolution fusion | flops 26901217280 | bytes 27530240 | tf_op jit(solution)/shard_map/bsf,fd->bsd/dot_general | solution.py:46
  1279.5 19.5 %copy.22 = bf16[2,2048,1280]{2,0,1:T(2,128)(2,1)S(1)} copy(bf16[2,2048,1280]{2,1,0:T(8,128)(2,1)} %convolution_convert_fusion) | data formatting | bytes 20971520 | tf_op jit(solution)/shard_map/convert_element_type | solution.py:24
  1299.0 119.5 %all_to_all.17 = bf16[2,2048,1280]{2,0,1:T(2,128)(2,1)} all-to-all(bf16[2,2048,1280]{2,0,1:T(2,128)(2,1)S(1)} %copy.22), channel_id=1, replica_groups=mesh['dp'=4,'tp'=4] {'tp'}, dimensions={1} | all-to-all | bytes 20971520 | tf_op jit(solution)/shard_map/all_to_all | solution.py:24
  1418.5 19.2 %convert_reduce_fusion = f32[2,512,1280]{2,0,1:T(2,128)S(1)} fusion(bf16[2,4,512,1280]{3,0,2,1:T(2,128)(2,1)} %bitcast.160), kind=kLoop, calls=%fused_computation.32 | loop fusion | flops 9175040 | bytes 15728640 | tf_op jit(solution)/shard_map/reduce_sum | solution.py:26
  1437.7 2.2 fusion.60
  (61 shorter events, 0.3 us)
Async XLA Ops:
  6.5 6.5 copy-start.1
  6.5 80.8 %all-gather.5.cloned.1.call-start = ((), (), s32[]{:S(2)}) async-start(), calls=%async_computation.4 | async-start | bytes 13107200 | tf_op jit(solution)/shard_map/all_gather | solution.py:37
  158.0 72.7 %copy-start.17 = (bf16[2,5,64,1280]{3,2,1,0:T(8,128)(2,1)S(1)}, bf16[2,5,64,1280]{3,2,1,0:T(8,128)(2,1)}, u32[]{:S(2)}) copy-start(bf16[2,5,64,1280]{3,2,1,0:T(8,128)(2,1)} %param.12) | copy-start | bytes 4915204
  313.1 6.2 copy-start.13
  313.1 121.4 %all-to-all-start = ((bf16[2,2048,1280]{2,0,1:T(2,128)(2,1)}), bf16[2,2048,1280]{2,0,1:T(2,128)(2,1)}, u32[]{:S(2)}, u32[]{:S(2)}) async-start(bf16[2,2048,1280]{2,0,1:T(2,128)(2,1)} %copy.15), calls=%async_computation | async-start | bytes 20971520 | tf_op jit(solution)/shard_map/all_to_all | solution.py:24
  319.2 208.2 %all-gather.7.cloned.1.call-start = ((), (), s32[]{:S(2)}) async-start(), calls=%async_computation.5 | async-start | bytes 13107200 | tf_op jit(solution)/shard_map/all_gather | solution.py:43
  434.5 19.2 %copy-start.2 = (bf16[2,512,1280]{2,1,0:T(8,128)(2,1)S(1)}, bf16[2,512,1280]{2,1,0:T(8,128)(2,1)}, u32[]{:S(2)}) copy-start(bf16[2,512,1280]{2,1,0:T(8,128)(2,1)} %param.9) | copy-start | bytes 7864324
  453.7 2.3 copy-start
  454.5 1.6 copy-start.10
  454.5 1.5 copy-start.11
  456.0 2.5 copy-start.14
  586.2 6.2 copy-start.15
  586.2 121.4 %all-to-all-start.1 = ((bf16[2,2048,1280]{2,0,1:T(2,128)(2,1)}), bf16[2,2048,1280]{2,0,1:T(2,128)(2,1)}, u32[]{:S(2)}, u32[]{:S(2)}) async-start(bf16[2,2048,1280]{2,0,1:T(2,128)(2,1)} %copy.17), calls=%async_computation.1 | async-start | bytes 20971520 | tf_op jit(solution)/shard_map/all_to_all | solution.py:24
  592.4 211.7 %all-gather.9.cloned.1.call-start = ((), (), s32[]{:S(2)}) async-start(), calls=%async_computation.6 | async-start | bytes 13107200 | tf_op jit(solution)/shard_map/all_gather | solution.py:37
  730.5 2.3 copy-start.3
  730.5 2.3 copy-start.8
  730.5 2.3 copy-start.9
  735.2 505.7 %all-gather.11.cloned.1.call-start = ((), (), s32[]{:S(2)}) async-start(), calls=%async_computation.7 | async-start | bytes 13107200 | tf_op jit(solution)/shard_map/all_gather | solution.py:43
  874.6 72.7 %copy-start.18 = (bf16[2,5,64,1280]{3,2,1,0:T(8,128)(2,1)S(1)}, bf16[2,5,64,1280]{3,2,1,0:T(8,128)(2,1)}, u32[]{:S(2)}) copy-start(bf16[2,5,64,1280]{3,2,1,0:T(8,128)(2,1)} %param.12) | copy-start | bytes 4915204
  955.6 208.5 %slice-start = ((s8[5242880]{0:T(1024)(128)(4,1)}), s8[4194304]{0:T(1024)(128)(4,1)S(1)}, s32[]{:S(2)}) async-start(s8[5242880]{0:T(1024)(128)(4,1)} %bitcast.155), calls=%async_computation.8 | async-start | bytes 8388608
  1030.5 133.6 %slice-start.1 = ((s8[5242880]{0:T(1024)(128)(4,1)}), s8[1048576]{0:T(1024)(128)(4,1)S(1)}, s32[]{:S(2)}) async-start(s8[5242880]{0:T(1024)(128)(4,1)} %bitcast.155), calls=%async_computation.9 | async-start | bytes 2097152
  1149.0 15.1 %copy-start.5 = (f32[1280]{0:T(1024)S(1)}, f32[1280]{0:T(1024)}, u32[]{:S(2)}) copy-start(f32[1280]{0:T(1024)} %get-tuple-element.17) | copy-start | bytes 15364
  1167.3 2.3 copy-start.4
  1167.3 2.3 copy-start.6
  1167.3 2.3 copy-start.7
  1169.6 71.3 %copy-start.16 = (f32[1280]{0:T(1024)S(1)}, f32[1280]{0:T(1024)}, u32[]{:S(2)}) copy-start(f32[1280]{0:T(1024)} %get-tuple-element.15) | copy-start | bytes 15364
  1279.4 158.2 %slice-start.2 = ((s8[5242880]{0:T(1024)(128)(4,1)}), s8[4194304]{0:T(1024)(128)(4,1)S(1)}, s32[]{:S(2)}) async-start(s8[5242880]{0:T(1024)(128)(4,1)} %bitcast.157), calls=%async_computation.10 | async-start | bytes 8388608
  1299.0 138.7 %slice-start.3 = ((s8[5242880]{0:T(1024)(128)(4,1)}), s8[1048576]{0:T(1024)(128)(4,1)S(1)}, s32[]{:S(2)}) async-start(s8[5242880]{0:T(1024)(128)(4,1)} %bitcast.157), calls=%async_computation.11 | async-start | bytes 2097152
  1418.5 19.2 %copy-start.12 = (f32[1280]{0:T(1024)S(1)}, f32[1280]{0:T(1024)}, u32[]{:S(2)}) copy-start(f32[1280]{0:T(1024)} %get-tuple-element.13) | copy-start | bytes 15364
Sparse Core Ops, SparseCore 0:
  15.7 71.5 all-gather.4
  458.6 68.7 all-gather.6
  735.3 68.7 all-gather.8
  1172.1 68.7 all-gather.10
where the time goes:
time: 1450 us
  waiting for transfers between devices  507 us (35%)
  matrix products  380 us (26%)
  blocking collectives  238 us (16%)
  local copies, waits for them, and re-layouts  196 us (14%)
  other arithmetic  99.3 us (7%)
    all_to_all x2, blocking collectives, reduce_rows(): lax.all_to_all(partial.astype(jnp.bfloat16), 'tp', 1, 0, tiled=True)  238 us
    all_to_all x2, waiting for transfers between devices, reduce_rows(): lax.all_to_all(partial.astype(jnp.bfloat16), 'tp', 1, 0, tiled=True)  229 us
    convert_element_type x4, local copies, waits for them, and re-layouts, reduce_rows(): partial.astype(jnp.bfloat16)  189 us
    dot_general x2, matrix products, attention(): jnp.einsum('bhqk,bkhe->bqhe', attn_prob, qkv_rows[:, :, 2], preferred_ele...  145 us
    all_gather x2, waiting for transfers between devices, local_layers(): full_rows = lax.all_gather(normed, 'tp', axis=1, tiled=True)  141 us
    all_gather x2, waiting for transfers between devices, local_layers(): full_rows2 = lax.all_gather(normed2, 'tp', axis=1, tiled=True)  137 us
    sub x2, matrix products, attention(): attn_prob = jax.nn.softmax(scores, axis=-1).astype(jnp.bfloat16)  110 us
    dot_general x2, matrix products, local_layers(): jnp.einsum('bsf,fd->bsd', gelu_out, w_down[layer_idx], preferred_element_...  77.2 us
  transfers between devices with their start and end apart: 6, of which 6 were waited for; matrix products, arithmetic and copies ran while one was open for 0% of the time, Pallas kernels for 0%

commit v1 on v0

v1 whole, which is shorter than its diff:
```python
import functools
import math

import jax
import jax.numpy as jnp
from jax import lax
from jax.experimental import pallas as pl
from jax.experimental.pallas import tpu as pltpu
from jax.sharding import PartitionSpec as P

LN_EPS = 1e-5
LOG2E = math.log2(math.e)
SWAP_CORE = [(0, 1), (1, 0), (2, 3), (3, 2)]
SWAP_CHIP = [(0, 2), (2, 0), (1, 3), (3, 1)]


def layer_norm(rows, gain, shift):
    row_mean = jnp.mean(rows, axis=-1, keepdims=True)
    centred = rows - row_mean
    row_var = jnp.mean(centred * centred, axis=-1, keepdims=True)
    return (centred * lax.rsqrt(row_var + LN_EPS) * gain + shift).astype(jnp.bfloat16)


def attn_kernel(q_ref, own_ref, peer_ref, out_ref, vext_ref, *, scale):
    n = own_ref.shape[0]
    bq = q_ref.shape[0]

    @pl.when(pl.program_id(0) == 0)
    def _():
        for i, col in enumerate((512, 640, 896)):
            vext_ref[i, :n, :128] = own_ref[:, col:col + 128]
            vext_ref[i, n:, :128] = peer_ref[:, col:col + 128]
            vext_ref[i, :, 128:] = jnp.ones((2 * n, 128), jnp.bfloat16)

    low = lax.broadcasted_iota(jnp.int32, (bq, 128), 1) < 64
    nt = (((1,), (1,)), ((), ()))
    outs = []
    for head in range(5):
        pair, odd = head // 2, head % 2
        if head < 4:
            q = q_ref[:, pair * 128:(pair + 1) * 128]
            q = jnp.where(low, jnp.zeros_like(q), q) if odd else jnp.where(low, q, jnp.zeros_like(q))
            kcol = 256 + pair * 128
        else:
            q = q_ref[:, 768:896]
            q = jnp.concatenate([jnp.zeros_like(q[:, :64]), q[:, :64]], axis=1)
            kcol = 768
        s_own = lax.dot_general(q, own_ref[:, kcol:kcol + 128], nt, preferred_element_type=jnp.float32)
        s_peer = lax.dot_general(q, peer_ref[:, kcol:kcol + 128], nt, preferred_element_type=jnp.float32)
        top = jnp.maximum(jnp.max(s_own, axis=1, keepdims=True), jnp.max(s_peer, axis=1, keepdims=True))
        p_own = jnp.exp2((s_own - top) * scale).astype(jnp.bfloat16)
        p_peer = jnp.exp2((s_peer - top) * scale).astype(jnp.bfloat16)
        o = jnp.dot(p_own, vext_ref[pair, :n, :], preferred_element_type=jnp.float32)
        o = o + jnp.dot(p_peer, vext_ref[pair, n:, :], preferred_element_type=jnp.float32)
        outs.append(o[:, :128] / o[:, 128:])
    out_ref[:, 0:128] = jnp.where(low, outs[0], outs[1]).astype(jnp.bfloat16)
    out_ref[:, 128:256] = jnp.where(low, outs[2], outs[3]).astype(jnp.bfloat16)
    out_ref[:, 256:320] = outs[4][:, :64].astype(jnp.bfloat16)


def attention(own, peer, block=512):
    n = own.shape[0]
    return pl.pallas_call(
        functools.partial(attn_kernel, scale=64 ** -0.5 * LOG2E),
        grid=(n // block,),
        in_specs=[
            pl.BlockSpec((block, 1024), lambda i: (i, 0)),
            pl.BlockSpec((n, 1024), lambda i: (0, 0)),
            pl.BlockSpec((n, 1024), lambda i: (0, 0)),
        ],
        out_specs=pl.BlockSpec((block, 320), lambda i: (i, 0)),
        out_shape=jax.ShapeDtypeStruct((n, 320), jnp.bfloat16),
        scratch_shapes=[pltpu.VMEM((3, 2 * n, 256), jnp.bfloat16)],
        compiler_params=pltpu.CompilerParams(vmem_limit_bytes=48 * 2 ** 20),
        cost_estimate=pl.CostEstimate(flops=5 * 4 * n * 2 * n * 256, bytes_accessed=6 * 2 ** 20, transcendentals=10 * n * n),
    )(own, own, peer)


def solution(mesh):
    def swap_core(a):
        return lax.ppermute(a, 'tp', SWAP_CORE)

    def swap_chip(a):
        return lax.ppermute(a, 'tp', SWAP_CHIP)

    def local_layers(hidden_in, norms, w_qkv, w_out, b_out, w_up, b_up, w_down, b_down):
        n_layers = w_qkv.shape[0]
        model = w_qkv.shape[1]
        chip = lax.axis_index('tp') // 2
        group = lax.axis_index('dp')
        n_groups = mesh.shape['dp']

        def far_of(a):
            rows = a.shape[0] // n_groups
            piece = lax.dynamic_slice_in_dim(a, group * rows, rows, 0)
            return lax.all_gather(swap_chip(piece), 'dp', axis=0, tiled=True)

        def four(own, gather=True):
            far = far_of(own) if gather else swap_chip(own)
            return [own, swap_core(own), far, swap_core(far)]

        kept = lax.dynamic_index_in_dim(hidden_in, chip, 0, keepdims=False)
        visiting = swap_chip(lax.dynamic_index_in_dim(hidden_in, 1 - chip, 0, keepdims=False))
        block = kept.shape[0]
        residual = jnp.concatenate([kept, visiting], axis=0).astype(jnp.float32)

        for l in range(n_layers):
            wt = jnp.transpose(w_qkv[l], (1, 2, 3, 0))
            wt = jnp.concatenate([wt[0, :4], wt[1, :4], wt[2, :4], wt[:, 4], jnp.zeros_like(wt[0, :1])], axis=0).reshape(1024, model)
            qkv_sh = four(wt)
            out_sh = four(w_out[l].reshape(-1, model), gather=False)
            up_sh = four(w_up[l])
            down_sh = four(w_down[l])
            bup_sh = four(b_up[l], gather=False)

            normed = layer_norm(residual, norms[l, 0], norms[l, 1])
            total = residual + b_out[l]
            qkv = [lax.dot_general(normed, w, (((1,), (1,)), ((), ())), preferred_element_type=jnp.float32).astype(jnp.bfloat16) for w in qkv_sh]
            for s in range(4):
                attn = attention(qkv[s], swap_core(qkv[s ^ 1]))
                total = total + jnp.dot(attn, out_sh[s], preferred_element_type=jnp.float32)
            residual = total

            def mlp(rows):
                normed2 = layer_norm(rows, norms[l, 2], norms[l, 3])
                acc = rows + b_down[l]
                for s in range(4):
                    u = jnp.dot(normed2, up_sh[s], preferred_element_type=jnp.float32) + bup_sh[s]
                    u = jax.nn.gelu(u, approximate=True).astype(jnp.bfloat16)
                    acc = acc + jnp.dot(u, down_sh[s], preferred_element_type=jnp.float32)
                return acc

            if l < n_layers - 1:
                residual = mlp(residual)
            else:
                back = swap_chip(mlp(residual[block:]).astype(jnp.bfloat16))
                stay = mlp(residual[:block]).astype(jnp.bfloat16)
        first = chip == 0
        return jnp.stack([jnp.where(first, stay, back), jnp.where(first, back, stay)])

    in_specs = (P('dp', 'tp', None), P(), P(None, None, None, 'tp', None), P(None, 'tp', None, None), P(), P(None, None, 'tp'), P(None, 'tp'), P(None, 'tp', None), P())
    return jax.shard_map(local_layers, mesh=mesh, in_specs=in_specs, out_specs=P('dp', 'tp', None), check_vma=False)
```

time: 1450 us -> 548 us (0.38)
  waiting for transfers between devices: 507 us -> 104 us
  blocking collectives: 238 us -> 0 us
  matrix products: 380 us -> 212 us
  local copies, waits for them, and re-layouts: 196 us -> 47.4 us
  Pallas kernels: 0 us -> 129 us
  other arithmetic: 99.3 us -> 11.1 us
    all_gather x4 -> x6, waiting for transfers between devices: 278 us -> 0.05 us  [far_of(): return lax.all_gather(swap_chip(piece), 'dp', axis=0, tiled=True)]
    all_to_all x2 -> x0, blocking collectives: 238 us -> none  [reduce_rows(): lax.all_to_all(partial.astype(jnp.bfloat16), 'tp', 1, 0, tiled=True)]
    all_to_all x2 -> x0, waiting for transfers between devices: 229 us -> none  [reduce_rows(): lax.all_to_all(partial.astype(jnp.bfloat16), 'tp', 1, 0, tiled=True)]
    convert_element_type x4 -> x0, local copies, waits for them, and re-layouts: 189 us -> none  [reduce_rows(): partial.astype(jnp.bfloat16)]
    pallas_call x0 -> x8, Pallas kernels: none -> 129 us  [attention(): pl.pallas_call(functools.partial(attn_kernel, scale=64 ** (-0.5) * LOG2E)...]
    sub x2 -> x0, matrix products: 110 us -> none  [attention(): attn_prob = jax.nn.softmax(scores, axis=-1).astype(jnp.bfloat16)]
    ppermute x0 -> x40, waiting for transfers between devices: none -> 104 us  [the longest x12 104 us: swap_chip(): return lax.ppermute(a, 'tp', SWAP_CHIP)]
    reduce_sum x4 -> x0, other arithmetic: 72.6 us -> none  [reduce_rows(): return jnp.sum(received.astype(jnp.float32), axis=0)]
  transfers between devices with their start and end apart: 6 -> 46, of which waited for: 6 -> 7; matrix products, arithmetic and copies ran while one was open for 0% -> 42% of each run, Pallas kernels for 0% -> 24%
where the time goes in v1:
time: 548 us; the launch traced here: 541 us
  matrix products  212 us (39%)
  Pallas kernels  129 us (24%)
  waiting for transfers between devices  104 us (19%)
  local copies, waits for them, and re-layouts  47.4 us (9%)
  starting transfers between devices  22.4 us (4%)
  between operations  14.6 us (3%)
  other arithmetic  11.1 us (2%)
    pallas_call x8, Pallas kernels, attention(): pl.pallas_call(functools.partial(attn_kernel, scale=64 ** (-0.5) * LOG2E)...  129 us
    dot_general x12, matrix products, mlp(): acc = acc + jnp.dot(u, down_sh[s], preferred_element_type=jnp.float32)  125 us
    ppermute x12, waiting for transfers between devices, swap_chip(): return lax.ppermute(a, 'tp', SWAP_CHIP)  104 us
    dot_general x8, matrix products, local_layers(): total = total + jnp.dot(attn, out_sh[s], preferred_element_type=jnp.float32)  46.4 us
    dot_general x8, matrix products, local_layers(): lax.dot_general(normed, w, (((1,), (1,)), ((), ())), preferred_element_ty...  40.8 us
    unnamed x79, local copies, waits for them, and re-layouts  18.2 us
    ppermute x12, starting transfers between devices, swap_chip(): return lax.ppermute(a, 'tp', SWAP_CHIP)  15.6 us
  transfers between devices with their start and end apart: 46, of which 7 were waited for; matrix products, arithmetic and copies ran while one was open for 42% of the time, Pallas kernels for 24%

profile of v1, /device:TPU:0, one launch (start us, length us, event | category | flops | bytes accessed | tf_op | source)
XLA Modules:
  0.0 541.1 jit_solution(17131110143665506877)
XLA Ops:
  15.6 3.3 collective-permute-start.5
  18.8 14.7 %collective-permute-done.5 = bf16[256,1280]{1,0:T(8,128)(2,1)S(1)} collective-permute-done((bf16[256,1280]{1,0:T(8,128)(2,1)S(1)}, bf16[256,1280]{1,0:T(8,128)(2,1)S(1)}, u32[]{:S(2)}, u32[]{:S(2)}) %collective-permute-start.5) | collective-permute-done | bytes 655392 | tf_op jit(solution)/shard_map/ppermute | solution.py:84
  34.5 5.8 %slice_bitcast_fusion.13 = (bf16[1280,1280]{1,0:T(8,128)(2,1)}, bf16[1280,1280]{1,0:T(8,128)(2,1)}, bf16[1,1280,1280]{2,1,0:T(8,128)(2,1)}, bf16[1,1280,1280]{2,1,0:T(8,128)(2,1)S(1)}) fusion(bf16[2,1280,1280]{2,1,0:T(8,128)(2,1)} %param.14), kind=kLoop, calls=%fused_computation.291 | loop fusion | bytes 19660800 | tf_op jit(solution)/shard_map/squeeze | solution.py:112
  42.1 17.7 %collective-permute-done.14 = bf16[320,1280]{1,0:T(8,128)(2,1)S(1)} collective-permute-done((bf16[320,1280]{1,0:T(8,128)(2,1)S(1)}, bf16[320,1280]{1,0:T(8,128)(2,1)S(1)}, u32[]{:S(2)}, u32[]{:S(2)}) %collective-permute-start.14) | collective-permute-done | bytes 819232 | tf_op jit(solution)/shard_map/ppermute | solution.py:84
  60.8 5.9 %slice_bitcast_fusion.12 = (bf16[1280,1280]{1,0:T(8,128)(2,1)}, bf16[1280,1280]{1,0:T(8,128)(2,1)}, bf16[1,1280,1280]{2,1,0:T(8,128)(2,1)}, bf16[1,1280,1280]{2,1,0:T(8,128)(2,1)S(1)}) fusion(bf16[2,1280,1280]{2,1,0:T(8,128)(2,1)} %param.16), kind=kLoop, calls=%fused_computation.288 | loop fusion | bytes 19660800 | tf_op jit(solution)/shard_map/squeeze | solution.py:113
  68.3 17.2 %collective-permute-done.16 = bf16[320,1280]{1,0:T(8,128)(2,1)S(1)} collective-permute-done((bf16[320,1280]{1,0:T(8,128)(2,1)S(1)}, bf16[320,1280]{1,0:T(8,128)(2,1)S(1)}, u32[]{:S(2)}, u32[]{:S(2)}) %collective-permute-start.16) | collective-permute-done | bytes 819232 | tf_op jit(solution)/shard_map/ppermute | solution.py:84
  91.1 3.0 dynamic-slice_bitcast_fusion.1
  94.9 12.6 %collective-permute-done.24 = bf16[256,1280]{1,0:T(8,128)(2,1)S(1)} collective-permute-done((bf16[256,1280]{1,0:T(8,128)(2,1)}, bf16[256,1280]{1,0:T(8,128)(2,1)S(1)}, u32[]{:S(2)}, u32[]{:S(2)}) %collective-permute-start.24) | collective-permute-done | bytes 655392 | tf_op jit(solution)/shard_map/ppermute | solution.py:84
  109.2 23.2 %collective-permute-done = bf16[512,1280]{1,0:T(8,128)(2,1)S(1)} collective-permute-done((bf16[512,1280]{1,0:T(8,128)(2,1)}, bf16[512,1280]{1,0:T(8,128)(2,1)S(1)}, u32[]{:S(2)}, u32[]{:S(2)}) %collective-permute-start) | collective-permute-done | bytes 1310752 | tf_op jit(solution)/shard_map/ppermute | solution.py:84
  133.6 5.1 convolution_convert_fusion.7.q_ref.own_ref
  147.5 13.7 %collective-permute-done.33 = bf16[320,1280]{1,0:T(8,128)(2,1)} collective-permute-done((bf16[320,1280]{1,0:T(8,128)(2,1)S(1)}, bf16[320,1280]{1,0:T(8,128)(2,1)}, u32[]{:S(2)}, u32[]{:S(2)}) %collective-permute-start.33) | collective-permute-done | bytes 819232 | tf_op jit(solution)/shard_map/ppermute | solution.py:84
  161.9 5.1 convolution_convert_fusion.6.q_ref.own_ref
  167.1 16.6 %shard_map.92 = bf16[1024,320]{1,0:T(8,128)(2,1)S(1)} custom-call(bf16[1024,1024]{1,0:T(8,128)(2,1)S(1)} %convolution_convert_fusion.6.q_ref.own_ref, bf16[1024,1024]{1,0:T(8,128)(2,1)S(1)} %convolution_convert_fusion.6.q_ref.own_ref, bf16[1024,1024]{1,0:T(8,128)(2,1)} %collective-permute-done.3.peer_ref), custom_call_target="tpu_custom_call" | custom-call | flops 10737418240 | bytes 6291456 | tf_op jit(solution)/shard_map/pallas_call | solution.py:63
  184.6 5.2 fusion.214
  189.8 4.5 convolution_convert_fusion.5.q_ref.own_ref
  194.6 7.3 %convolution_convert_fusion.4.q_ref.own_ref = bf16[1024,1024]{1,0:T(8,128)(2,1)} fusion(bf16[1024,1280]{1,0:T(8,128)(2,1)} %collective-permute-done.6, f32[1280]{0:T(1024)S(1)} %get-tuple-element.12, f32[1280]{0:T(1024)S(1)} %get-tuple-element.13, f32[1024]{0:T(1024)S(1)} %add_rsqrt_fusion.2, f32[1024]{0:T(1024)S(1)} %broadcast_multiply_fusion.2, ...), kind=kOutput, calls=%fused_computation.163 | convolution fusion | flops 2697199616 | bytes 7358464 | tf_op jit(solution)/shard_map/dot_general | solution.py:118
  202.2 14.8 %shard_map.91 = bf16[1024,320]{1,0:T(8,128)(2,1)S(1)} custom-call(bf16[1024,1024]{1,0:T(8,128)(2,1)S(1)} %convolution_convert_fusion.7.q_ref.own_ref, bf16[1024,1024]{1,0:T(8,128)(2,1)S(1)} %convolution_convert_fusion.7.q_ref.own_ref, bf16[1024,1024]{1,0:T(8,128)(2,1)S(1)} %collective-permute-done.2.peer_ref), custom_call_target="tpu_custom_call" | custom-call | flops 10737418240 | bytes 6291456 | tf_op jit(solution)/shard_map/pallas_call | solution.py:63
  217.0 5.0 fusion.213
  225.2 17.4 %shard_map.94 = bf16[1024,320]{1,0:T(8,128)(2,1)S(1)} custom-call(bf16[1024,1024]{1,0:T(8,128)(2,1)} %convolution_convert_fusion.4.q_ref.own_ref, bf16[1024,1024]{1,0:T(8,128)(2,1)} %convolution_convert_fusion.4.q_ref.own_ref, bf16[1024,1024]{1,0:T(8,128)(2,1)S(1)} %copy-done.3), custom_call_target="tpu_custom_call" | custom-call | flops 10737418240 | bytes 6291456 | tf_op jit(solution)/shard_map/pallas_call | solution.py:63
  243.2 15.0 %shard_map.93 = bf16[1024,320]{1,0:T(8,128)(2,1)S(1)} custom-call(bf16[1024,1024]{1,0:T(8,128)(2,1)S(1)} %convolution_convert_fusion.5.q_ref.own_ref, bf16[1024,1024]{1,0:T(8,128)(2,1)S(1)} %convolution_convert_fusion.5.q_ref.own_ref, bf16[1024,1024]{1,0:T(8,128)(2,1)S(1)} %collective-permute-done.7.peer_ref), custom_call_target="tpu_custom_call" | custom-call | flops 10737418240 | bytes 6291456 | tf_op jit(solution)/shard_map/pallas_call | solution.py:63
  258.2 5.1 fusion.215
  263.5 8.2 %fusion.209 = (f32[1024]{0:T(1024)S(1)}, f32[1024,1280]{1,0:T(8,128)S(1)}) fusion(bf16[1024,320]{1,0:T(8,128)(2,1)S(1)} %shard_map.94, bf16[320,1280]{1,0:T(8,128)(2,1)} %collective-permute-done.10, f32[1024,1280]{1,0:T(8,128)} %fusion.215, f32[1024,1280]{1,0:T(8,128)} %fusion.214, f32[1024,1280]{1,0:T(8,128)} %fusion.213, ...), kind=kOutput, calls=%fused_computation.293 | convolution fusion | flops 851966976 | bytes 25076736 | tf_op jit(solution)/shard_map/dot_general | solution.py:121
  275.0 12.5 %fusion.123 = f32[1024,1280]{1,0:T(8,128)} fusion(bf16[1024,1280]{1,0:T(8,128)(2,1)S(1)} %add_convert_fusion.1, f32[1280]{0:T(1024)S(1)} %get-tuple-element.18, bf16[2,1280,1280]{2,1,0:T(8,128)(2,1)} %param.16, bf16[2,1280,1280]{2,1,0:T(8,128)(2,1)} %param.14), kind=kOutput, calls=%fused_computation.173 | convolution fusion | flops 6723993600 | bytes 14423040 | tf_op jit(solution)/shard_map/dot_general | solution.py:130
  287.8 12.4 %fusion.121 = f32[1024,1280]{1,0:T(8,128)} fusion(bf16[1280,1280]{1,0:T(8,128)(2,1)} %all-gather.11.cloned.1.call-done, bf16[1024,1280]{1,0:T(8,128)(2,1)S(1)} %add_convert_fusion.1, bf16[1280,1280]{1,0:T(8,128)(2,1)} %all-gather.9.cloned.1.call-done, f32[1280]{0:T(1024)S(1)} %collective-permute-done.15), kind=kOutput, calls=%fused_computation.171 | convolution fusion | flops 6723993600 | bytes 14423040 | tf_op jit(solution)/shard_map/dot_general | solution.py:130
  301.5 12.8 %fusion.122 = f32[1024,1280]{1,0:T(8,128)} fusion(bf16[1280,1280]{1,0:T(8,128)(2,1)} %collective-permute-done.13, bf16[1024,1280]{1,0:T(8,128)(2,1)S(1)} %add_convert_fusion.1, bf16[1280,1280]{1,0:T(8,128)(2,1)} %collective-permute-done.11, f32[1280]{0:T(1024)S(1)} %collective-permute-done.12), kind=kOutput, calls=%fused_computation.172 | convolution fusion | flops 6723993600 | bytes 14423040 | tf_op jit(solution)/shard_map/dot_general | solution.py:130
  314.7 15.9 %fusion.210 = (f32[1024]{0:T(1024)S(1)}, f32[1024,1280]{1,0:T(8,128)}) fusion(bf16[1280,1280]{1,0:T(8,128)(2,1)} %collective-permute-done.19, f32[1280]{0:T(1024)S(1)} %collective-permute-done.18, f32[1024,1280]{1,0:T(8,128)} %fusion.121, f32[1024,1280]{1,0:T(8,128)} %fusion.122, f32[1024,1280]{1,0:T(8,128)} %fusion.123, f32[1024,1280]{1,0:T(8,128)} %copy-done.8, ...), kind=kOutput, calls=%fused_computation.294 | convolution fusion | flops 6731856896 | bytes 35403776 | tf_op jit(solution)/shard_map/dot_general | solution.py:130
  330.6 3.3 multiply_reduce_fusion
  335.6 6.0 %convolution_convert_fusion.2.q_ref.own_ref = bf16[1024,1024]{1,0:T(8,128)(2,1)S(1)} fusion(bf16[1024,1280]{1,0:T(8,128)(2,1)S(1)} %add_convert_fusion, bf16[1024,1280]{1,0:T(8,128)(2,1)} %collective-permute-done.20), kind=kOutput, calls=%fused_computation.161 | convolution fusion | flops 2685403136 | bytes 7340032 | tf_op jit(solution)/shard_map/dot_general | solution.py:118
  344.3 5.6 %convolution_convert_fusion.q_ref.own_ref = bf16[1024,1024]{1,0:T(8,128)(2,1)S(1)} fusion(bf16[1024,1280]{1,0:T(8,128)(2,1)} %copy-done.13, bf16[1024,1280]{1,0:T(8,128)(2,1)} %collective-permute-done.25), kind=kOutput, calls=%fused_computation.159 | convolution fusion | flops 2685403136 | bytes 7340032 | tf_op jit(solution)/shard_map/dot_general | solution.py:118
  349.9 3.1 convolution_convert_fusion.3.q_ref.own_ref
  353.1 4.1 convolution_convert_fusion.1.q_ref.own_ref
  357.7 16.4 %shard_map.95 = bf16[1024,320]{1,0:T(8,128)(2,1)S(1)} custom-call(bf16[1024,1024]{1,0:T(8,128)(2,1)S(1)} %convolution_convert_fusion.3.q_ref.own_ref, bf16[1024,1024]{1,0:T(8,128)(2,1)S(1)} %convolution_convert_fusion.3.q_ref.own_ref, bf16[1024,1024]{1,0:T(8,128)(2,1)} %collective-permute-done.21.peer_ref), custom_call_target="tpu_custom_call" | custom-call | flops 10737418240 | bytes 6291456 | tf_op jit(solution)/shard_map/pallas_call | solution.py:63
  377.1 17.2 %shard_map.97 = bf16[1024,320]{1,0:T(8,128)(2,1)S(1)} custom-call(bf16[1024,1024]{1,0:T(8,128)(2,1)} %convolution_convert_fusion.1.q_ref.own_ref, bf16[1024,1024]{1,0:T(8,128)(2,1)} %convolution_convert_fusion.1.q_ref.own_ref, bf16[1024,1024]{1,0:T(8,128)(2,1)S(1)} %copy-done.5), custom_call_target="tpu_custom_call" | custom-call | flops 10737418240 | bytes 6291456 | tf_op jit(solution)/shard_map/pallas_call | solution.py:63
  394.3 3.8 fusion.216
  398.6 5.0 fusion.218
  404.2 15.2 %shard_map.96 = bf16[1024,320]{1,0:T(8,128)(2,1)S(1)} custom-call(bf16[1024,1024]{1,0:T(8,128)(2,1)S(1)} %convolution_convert_fusion.2.q_ref.own_ref, bf16[1024,1024]{1,0:T(8,128)(2,1)S(1)} %convolution_convert_fusion.2.q_ref.own_ref, bf16[1024,1024]{1,0:T(8,128)(2,1)S(1)} %collective-permute-done.22.peer_ref), custom_call_target="tpu_custom_call" | custom-call | flops 10737418240 | bytes 6291456 | tf_op jit(solution)/shard_map/pallas_call | solution.py:63
  419.5 5.1 fusion.217
  425.1 16.6 %shard_map.98 = bf16[1024,320]{1,0:T(8,128)(2,1)S(1)} custom-call(bf16[1024,1024]{1,0:T(8,128)(2,1)S(1)} %copy-done.1, bf16[1024,1024]{1,0:T(8,128)(2,1)S(1)} %copy-done.1, bf16[1024,1024]{1,0:T(8,128)(2,1)} %collective-permute-done.28.peer_ref), custom_call_target="tpu_custom_call" | custom-call | flops 10737418240 | bytes 6291456 | tf_op jit(solution)/shard_map/pallas_call | solution.py:63
  441.8 9.0 %add_add_fusion = f32[1024,1280]{1,0:T(8,128)S(1)} fusion(f32[1024,1280]{1,0:T(8,128)} %fusion.218, f32[1024,1280]{1,0:T(8,128)} %fusion.217, f32[1024,1280]{1,0:T(8,128)} %fusion.216, f32[1024,1280]{1,0:T(8,128)} %get-tuple-element.42, bf16[1024,320]{1,0:T(8,128)(2,1)S(1)} %shard_map.98, bf16[320,1280]{1,0:T(8,128)(2,1)} %collective-permute-done.29, ...), kind=kOutput, calls=%fused_computation.49 | convolution fusion | flops 845414400 | bytes 27694080 | tf_op jit(solution)/shard_map/dot_general | solution.py:121
  454.4 8.7 %fusion.126 = f32[512,1280]{1,0:T(8,128)} fusion(bf16[512,1280]{1,0:T(8,128)(2,1)S(1)} %get-tuple-element.30, f32[1280]{0:T(1024)S(1)} %copy-done.33, bf16[2,1280,1280]{2,1,0:T(8,128)(2,1)} %param.16, bf16[2,1280,1280]{2,1,0:T(8,128)(2,1)} %param.14), kind=kOutput, calls=%fused_computation.180 | convolution fusion | flops 3361996800 | bytes 10490880 | tf_op jit(solution)/shard_map/dot_general | solution.py:130
  463.1 8.2 %fusion.125 = f32[512,1280]{1,0:T(8,128)} fusion(bf16[1280,1280]{1,0:T(8,128)(2,1)} %all-gather.17.cloned.1.call-done, bf16[512,1280]{1,0:T(8,128)(2,1)S(1)} %get-tuple-element.30, bf16[1280,1280]{1,0:T(8,128)(2,1)} %all-gather.15.cloned.1.call-done, f32[1280]{0:T(1024)S(1)} %collective-permute-done.34), kind=kOutput, calls=%fused_computation.179 | convolution fusion | flops 3361996800 | bytes 10490880 | tf_op jit(solution)/shard_map/dot_general | solution.py:130
  471.7 8.2 %fusion.124 = f32[512,1280]{1,0:T(8,128)} fusion(bf16[1280,1280]{1,0:T(8,128)(2,1)} %collective-permute-done.38, bf16[512,1280]{1,0:T(8,128)(2,1)S(1)} %get-tuple-element.30, bf16[1280,1280]{1,0:T(8,128)(2,1)} %collective-permute-done.36, f32[1280]{0:T(1024)S(1)} %collective-permute-done.37), kind=kOutput, calls=%fused_computation.178 | convolution fusion | flops 3361996800 | bytes 10490880 | tf_op jit(solution)/shard_map/dot_general | solution.py:130
  480.0 10.8 %fusion.47 = bf16[512,1280]{1,0:T(8,128)(2,1)} fusion(f32[512,1280]{1,0:T(8,128)} %fusion.124, f32[512,1280]{1,0:T(8,128)} %fusion.125, bf16[1280,1280]{1,0:T(8,128)(2,1)} %collective-permute-done.32, f32[512,1280]{1,0:T(8,128)} %fusion.126, f32[1024,1280]{1,0:T(8,128)} %copy-done.6, f32[1280]{0:T(1024)S(1)} %copy-done.32, ...), kind=kOutput, calls=%fused_computation.78 | convolution fusion | flops 3365928960 | bytes 19671040 | tf_op jit(solution)/shard_map/dot_general | solution.py:130
  491.9 8.5 %fusion.129 = f32[512,1280]{1,0:T(8,128)} fusion(bf16[512,1280]{1,0:T(8,128)(2,1)S(1)} %get-tuple-element.29, f32[1280]{0:T(1024)S(1)} %copy-done.33, bf16[2,1280,1280]{2,1,0:T(8,128)(2,1)} %param.16, bf16[2,1280,1280]{2,1,0:T(8,128)(2,1)} %param.14), kind=kOutput, calls=%fused_computation.183 | convolution fusion | flops 3361996800 | bytes 10490880 | tf_op jit(solution)/shard_map/dot_general | solution.py:130
  500.4 8.2 %fusion.128 = f32[512,1280]{1,0:T(8,128)} fusion(bf16[1280,1280]{1,0:T(8,128)(2,1)} %all-gather.17.cloned.1.call-done, bf16[512,1280]{1,0:T(8,128)(2,1)S(1)} %get-tuple-element.29, bf16[1280,1280]{1,0:T(8,128)(2,1)} %all-gather.15.cloned.1.call-done, f32[1280]{0:T(1024)S(1)} %collective-permute-done.34), kind=kOutput, calls=%fused_computation.182 | convolution fusion | flops 3361996800 | bytes 10490880 | tf_op jit(solution)/shard_map/dot_general | solution.py:130
  508.6 8.2 %fusion.127 = f32[512,1280]{1,0:T(8,128)} fusion(bf16[1280,1280]{1,0:T(8,128)(2,1)} %collective-permute-done.38, bf16[512,1280]{1,0:T(8,128)(2,1)S(1)} %get-tuple-element.29, bf16[1280,1280]{1,0:T(8,128)(2,1)} %collective-permute-done.36, f32[1280]{0:T(1024)S(1)} %collective-permute-done.37), kind=kOutput, calls=%fused_computation.181 | convolution fusion | flops 3361996800 | bytes 10490880 | tf_op jit(solution)/shard_map/dot_general | solution.py:130
  516.8 4.7 collective-permute-done.39
  521.5 10.6 %select_bitcast_fusion.1 = (bf16[1,512,1280]{2,1,0:T(8,128)(2,1)S(1)}, bf16[1,512,1280]{2,1,0:T(8,128)(2,1)S(1)}) fusion(bf16[512,1280]{1,0:T(8,128)(2,1)} %collective-permute-done.39, pred[]{:T(512)S(6)} %eq.3, f32[512,1280]{1,0:T(8,128)} %fusion.127, f32[512,1280]{1,0:T(8,128)} %fusion.128, bf16[1280,1280]{1,0:T(8,128)(2,1)} %collective-permute-done.32, ...), kind=kOutput, calls=%fused_computation.168 | convolution fusion | flops 3367239680 | bytes 22292480 | tf_op jit(solution)/shard_map/dot_general | solution.py:130
  (203 shorter events, 59.9 us)
Async XLA Ops:
  6.5 154.9 %all-gather.7.cloned.1.call-start = ((), (), s32[]{:S(2)}) async-start(), calls=%async_computation | async-start | bytes 3276800 | tf_op jit(solution)/shard_map/all_gather | solution.py:96
  15.6 18.0 %collective-permute-start.5 = (bf16[256,1280]{1,0:T(8,128)(2,1)S(1)}, bf16[256,1280]{1,0:T(8,128)(2,1)S(1)}, u32[]{:S(2)}, u32[]{:S(2)}) collective-permute-start(bf16[256,1280]{1,0:T(8,128)(2,1)S(1)} %constant_dynamic-slice_fusion.1), channel_id=1, source_target_pairs={{0,2},{2,0},{1,3},{3,1},{4,6},{6,4},{5,7},{7,5},{8,10},{10,8},{9,1... | collective-permute-start | bytes 1966088 | tf_op jit(solution)/shard_map/ppermute | solution.py:84
  34.4 228.9 %all-gather.9.cloned.1.call-start = ((), (), s32[]{:S(2)}) async-start(), calls=%async_computation.1 | async-start | bytes 4096000 | tf_op jit(solution)/shard_map/all_gather | solution.py:96
  40.4 19.4 %collective-permute-start.14 = (bf16[320,1280]{1,0:T(8,128)(2,1)S(1)}, bf16[320,1280]{1,0:T(8,128)(2,1)S(1)}, u32[]{:S(2)}, u32[]{:S(2)}) collective-permute-start(bf16[320,1280]{1,0:T(8,128)(2,1)S(1)} %dynamic-slice_bitcast_fusion.5), channel_id=1, source_target_pairs={{0,2},{2,0},{1,3},{3,1},{4,6},{6,4},{5,7},{7,5},{8,10},{10,8},{9,1... | collective-permute-start | bytes 2457608 | tf_op jit(solution)/shard_map/ppermute | solution.py:84
  60.8 226.7 %all-gather.11.cloned.1.call-start = ((), (), s32[]{:S(2)}) async-start(), calls=%async_computation.2 | async-start | bytes 4096000 | tf_op jit(solution)/shard_map/all_gather | solution.py:96
  66.8 18.7 %collective-permute-start.16 = (bf16[320,1280]{1,0:T(8,128)(2,1)S(1)}, bf16[320,1280]{1,0:T(8,128)(2,1)S(1)}, u32[]{:S(2)}, u32[]{:S(2)}) collective-permute-start(bf16[320,1280]{1,0:T(8,128)(2,1)S(1)} %dynamic-slice_bitcast_fusion.4), channel_id=1, source_target_pairs={{0,2},{2,0},{1,3},{3,1},{4,6},{6,4},{5,7},{7,5},{8,10},{10,8},{9,1... | collective-permute-start | bytes 2457608 | tf_op jit(solution)/shard_map/ppermute | solution.py:84
  86.4 228.0 %all-gather.13.cloned.1.call-start = ((), (), s32[]{:S(2)}) async-start(), calls=%async_computation.3 | async-start | bytes 3276800 | tf_op jit(solution)/shard_map/all_gather | solution.py:96
  89.9 17.6 %collective-permute-start.24 = (bf16[256,1280]{1,0:T(8,128)(2,1)}, bf16[256,1280]{1,0:T(8,128)(2,1)S(1)}, u32[]{:S(2)}, u32[]{:S(2)}) collective-permute-start(bf16[256,1280]{1,0:T(8,128)(2,1)} %constant_dynamic-slice_fusion), channel_id=1, source_target_pairs={{0,2},{2,0},{1,3},{3,1},{4,6},{6,4},{5,7},{7,5},{8,10},{10,8},{9,1... | collective-permute-start | bytes 1966088 | tf_op jit(solution)/shard_map/ppermute | solution.py:84
  91.1 17.4 %copy-start.23 = (f32[2,4,1280]{2,1,0:T(4,128)S(1)}, f32[2,4,1280]{2,1,0:T(4,128)}, u32[]{:S(2)}) copy-start(f32[2,4,1280]{2,1,0:T(4,128)} %param.10) | copy-start | bytes 122884
  94.0 38.3 %collective-permute-start = (bf16[512,1280]{1,0:T(8,128)(2,1)}, bf16[512,1280]{1,0:T(8,128)(2,1)S(1)}, u32[]{:S(2)}, u32[]{:S(2)}) collective-permute-start(bf16[512,1280]{1,0:T(8,128)(2,1)} %get-tuple-element.36), channel_id=1, source_target_pairs={{0,2},{2,0},{1,3},{3,1},{4,6},{6,4},{5,7},{7,5},{8,10},{10,8},{9,1... | collective-permute-start | bytes 3932168 | tf_op jit(solution)/shard_map/ppermute | solution.py:84
  108.3 316.2 %all-gather.15.cloned.1.call-start = ((), (), s32[]{:S(2)}) async-start(), calls=%async_computation.4 | async-start | bytes 4096000 | tf_op jit(solution)/shard_map/all_gather | solution.py:96
  108.4 53.0 %collective-permute-start.1 = (bf16[1024,1280]{1,0:T(8,128)(2,1)}, bf16[1024,1280]{1,0:T(8,128)(2,1)}, u32[]{:S(2)}, u32[]{:S(2)}) collective-permute-start(bf16[1024,1280]{1,0:T(8,128)(2,1)} %bitcast.9), channel_id=1, source_target_pairs={{0,1},{1,0},{2,3},{3,2},{4,5},{5,4},{6,7},{7,6},{8,9},{9,8},{10,11... | collective-permute-start | bytes 7864328 | tf_op jit(solution)/shard_map/ppermute | solution.py:81
  138.8 28.3 %collective-permute-start.3 = (bf16[1024,1024]{1,0:T(8,128)(2,1)S(1)}, bf16[1024,1024]{1,0:T(8,128)(2,1)}, u32[]{:S(2)}, u32[]{:S(2)}) collective-permute-start(bf16[1024,1024]{1,0:T(8,128)(2,1)S(1)} %convolution_convert_fusion.7.q_ref.own_ref), channel_id=1, source_target_pairs={{0,1},{1,0},{2,3},{3,2},{4,5},{5,4},{6,7},{7,6},{8,9},{9,8},{10,11... | collective-permute-start | bytes 6291464 | tf_op jit(solution)/shard_map/ppermute | solution.py:81
  140.1 21.2 %collective-permute-start.33 = (bf16[320,1280]{1,0:T(8,128)(2,1)S(1)}, bf16[320,1280]{1,0:T(8,128)(2,1)}, u32[]{:S(2)}, u32[]{:S(2)}) collective-permute-start(bf16[320,1280]{1,0:T(8,128)(2,1)S(1)} %dynamic-slice_bitcast_fusion.3), channel_id=1, source_target_pairs={{0,2},{2,0},{1,3},{3,1},{4,6},{6,4},{5,7},{7,5},{8,10},{10,8},{9,1... | collective-permute-start | bytes 2457608 | tf_op jit(solution)/shard_map/ppermute | solution.py:84
  142.4 41.3 %collective-permute-start.4 = (bf16[320,1280]{1,0:T(8,128)(2,1)}, bf16[320,1280]{1,0:T(8,128)(2,1)}, u32[]{:S(2)}, u32[]{:S(2)}) collective-permute-start(bf16[320,1280]{1,0:T(8,128)(2,1)} %bitcast.10), channel_id=1, source_target_pairs={{0,1},{1,0},{2,3},{3,2},{4,5},{5,4},{6,7},{7,6},{8,9},{9,8},{10,11... | collective-permute-start | bytes 2457608 | tf_op jit(solution)/shard_map/ppermute | solution.py:81
  142.5 100.2 %collective-permute-start.8 = (bf16[320,1280]{1,0:T(8,128)(2,1)}, bf16[320,1280]{1,0:T(8,128)(2,1)}, u32[]{:S(2)}, u32[]{:S(2)}) collective-permute-start(bf16[320,1280]{1,0:T(8,128)(2,1)} %bitcast.10), channel_id=1, source_target_pairs={{0,2},{2,0},{1,3},{3,1},{4,6},{6,4},{5,7},{7,5},{8,10},{10,8},{9,1... | collective-permute-start | bytes 2457608 | tf_op jit(solution)/shard_map/ppermute | solution.py:84
  161.3 138.9 %collective-permute-start.12 = (f32[1280]{0:T(1024)S(1)}, f32[1280]{0:T(1024)S(1)}, u32[]{:S(2)}, u32[]{:S(2)}) collective-permute-start(f32[1280]{0:T(1024)S(1)} %get-tuple-element.18), channel_id=1, source_target_pairs={{0,1},{1,0},{2,3},{3,2},{4,5},{5,4},{6,7},{7,6},{8,9},{9,8},{10,11... | collective-permute-start | bytes 15368 | tf_op jit(solution)/shard_map/ppermute | solution.py:81
  161.3 280.4 %all-gather.17.cloned.1.call-start = ((), (), s32[]{:S(2)}) async-start(), calls=%async_computation.5 | async-start | bytes 4096000 | tf_op jit(solution)/shard_map/all_gather | solution.py:96
  161.4 32.9 %collective-permute-start.6 = (bf16[1024,1280]{1,0:T(8,128)(2,1)}, bf16[1024,1280]{1,0:T(8,128)(2,1)}, u32[]{:S(2)}, u32[]{:S(2)}) collective-permute-start(bf16[1024,1280]{1,0:T(8,128)(2,1)} %all-gather.7.cloned.1.call-done), channel_id=1, source_target_pairs={{0,1},{1,0},{2,3},{3,2},{4,5},{5,4},{6,7},{7,6},{8,9},{9,8},{10,11... | collective-permute-start | bytes 7864328 | tf_op jit(solution)/shard_map/ppermute | solution.py:81
  167.0 35.0 %collective-permute-start.2 = (bf16[1024,1024]{1,0:T(8,128)(2,1)S(1)}, bf16[1024,1024]{1,0:T(8,128)(2,1)S(1)}, u32[]{:S(2)}, u32[]{:S(2)}) collective-permute-start(bf16[1024,1024]{1,0:T(8,128)(2,1)S(1)} %convolution_convert_fusion.6.q_ref.own_ref), channel_id=1, source_target_pairs={{0,1},{1,0},{2,3},{3,2},{4,5},{5,4},{6,7},{7,6},{8,9},{9,8},{10,11... | collective-permute-start | bytes 6291464 | tf_op jit(solution)/shard_map/ppermute | solution.py:81
  183.7 103.8 %collective-permute-start.15 = (f32[1280]{0:T(1024)S(1)}, f32[1280]{0:T(1024)S(1)}, u32[]{:S(2)}, u32[]{:S(2)}) collective-permute-start(f32[1280]{0:T(1024)S(1)} %get-tuple-element.18), channel_id=1, source_target_pairs={{0,2},{2,0},{1,3},{3,1},{4,6},{6,4},{5,7},{7,5},{8,10},{10,8},{9,1... | collective-permute-start | bytes 15368 | tf_op jit(solution)/shard_map/ppermute | solution.py:84
  194.3 27.8 %collective-permute-start.9 = (bf16[1024,1024]{1,0:T(8,128)(2,1)S(1)}, bf16[1024,1024]{1,0:T(8,128)(2,1)S(1)}, u32[]{:S(2)}, u32[]{:S(2)}) collective-permute-start(bf16[1024,1024]{1,0:T(8,128)(2,1)S(1)} %convolution_convert_fusion.5.q_ref.own_ref), channel_id=1, source_target_pairs={{0,1},{1,0},{2,3},{3,2},{4,5},{5,4},{6,7},{7,6},{8,9},{9,8},{10,11... | collective-permute-start | bytes 6291464 | tf_op jit(solution)/shard_map/ppermute | solution.py:81
  202.0 40.9 %collective-permute-start.7 = (bf16[1024,1024]{1,0:T(8,128)(2,1)}, bf16[1024,1024]{1,0:T(8,128)(2,1)S(1)}, u32[]{:S(2)}, u32[]{:S(2)}) collective-permute-start(bf16[1024,1024]{1,0:T(8,128)(2,1)} %convolution_convert_fusion.4.q_ref.own_ref), channel_id=1, source_target_pairs={{0,1},{1,0},{2,3},{3,2},{4,5},{5,4},{6,7},{7,6},{8,9},{9,8},{10,11... | collective-permute-start | bytes 6291464 | tf_op jit(solution)/shard_map/ppermute | solution.py:81
  223.4 77.1 %collective-permute-start.11 = (bf16[1280,1280]{1,0:T(8,128)(2,1)}, bf16[1280,1280]{1,0:T(8,128)(2,1)}, u32[]{:S(2)}, u32[]{:S(2)}) collective-permute-start(bf16[1280,1280]{1,0:T(8,128)(2,1)} %get-tuple-element.22), channel_id=1, source_target_pairs={{0,1},{1,0},{2,3},{3,2},{4,5},{5,4},{6,7},{7,6},{8,9},{9,8},{10,11... | collective-permute-start | bytes 9830408 | tf_op jit(solution)/shard_map/ppermute | solution.py:81
  242.7 58.7 %collective-permute-start.13 = (bf16[1280,1280]{1,0:T(8,128)(2,1)}, bf16[1280,1280]{1,0:T(8,128)(2,1)}, u32[]{:S(2)}, u32[]{:S(2)}) collective-permute-start(bf16[1280,1280]{1,0:T(8,128)(2,1)} %get-tuple-element.26), channel_id=1, source_target_pairs={{0,1},{1,0},{2,3},{3,2},{4,5},{5,4},{6,7},{7,6},{8,9},{9,8},{10,11... | collective-permute-start | bytes 9830408 | tf_op jit(solution)/shard_map/ppermute | solution.py:81
  242.9 20.4 %collective-permute-start.10 = (bf16[320,1280]{1,0:T(8,128)(2,1)}, bf16[320,1280]{1,0:T(8,128)(2,1)}, u32[]{:S(2)}, u32[]{:S(2)}) collective-permute-start(bf16[320,1280]{1,0:T(8,128)(2,1)} %collective-permute-done.8), channel_id=1, source_target_pairs={{0,1},{1,0},{2,3},{3,2},{4,5},{5,4},{6,7},{7,6},{8,9},{9,8},{10,11... | collective-permute-start | bytes 2457608 | tf_op jit(solution)/shard_map/ppermute | solution.py:81
  263.3 51.4 %collective-permute-start.17 = (bf16[1280,1280]{1,0:T(8,128)(2,1)}, bf16[1280,1280]{1,0:T(8,128)(2,1)}, u32[]{:S(2)}, u32[]{:S(2)}) collective-permute-start(bf16[1280,1280]{1,0:T(8,128)(2,1)} %all-gather.9.cloned.1.call-done), channel_id=1, source_target_pairs={{0,1},{1,0},{2,3},{3,2},{4,5},{5,4},{6,7},{7,6},{8,9},{9,8},{10,11... | collective-permute-start | bytes 9830408 | tf_op jit(solution)/shard_map/ppermute | solution.py:81
  287.5 27.2 %collective-permute-start.19 = (bf16[1280,1280]{1,0:T(8,128)(2,1)}, bf16[1280,1280]{1,0:T(8,128)(2,1)}, u32[]{:S(2)}, u32[]{:S(2)}) collective-permute-start(bf16[1280,1280]{1,0:T(8,128)(2,1)} %all-gather.11.cloned.1.call-done), channel_id=1, source_target_pairs={{0,1},{1,0},{2,3},{3,2},{4,5},{5,4},{6,7},{7,6},{8,9},{9,8},{10,11... | collective-permute-start | bytes 9830408 | tf_op jit(solution)/shard_map/ppermute | solution.py:81
  300.2 35.4 %collective-permute-start.20 = (bf16[1024,1280]{1,0:T(8,128)(2,1)}, bf16[1024,1280]{1,0:T(8,128)(2,1)}, u32[]{:S(2)}, u32[]{:S(2)}) collective-permute-start(bf16[1024,1280]{1,0:T(8,128)(2,1)} %bitcast.145), channel_id=1, source_target_pairs={{0,1},{1,0},{2,3},{3,2},{4,5},{5,4},{6,7},{7,6},{8,9},{9,8},{10,11... | collective-permute-start | bytes 7864328 | tf_op jit(solution)/shard_map/ppermute | solution.py:81
  300.4 42.9 %collective-permute-start.35 = (bf16[320,1280]{1,0:T(8,128)(2,1)}, bf16[320,1280]{1,0:T(8,128)(2,1)}, u32[]{:S(2)}, u32[]{:S(2)}) collective-permute-start(bf16[320,1280]{1,0:T(8,128)(2,1)} %dynamic-slice_bitcast_fusion.2), channel_id=1, source_target_pairs={{0,2},{2,0},{1,3},{3,1},{4,6},{6,4},{5,7},{7,5},{8,10},{10,8},{9,1... | collective-permute-start | bytes 2457608 | tf_op jit(solution)/shard_map/ppermute | solution.py:84
  301.3 13.0 %collective-permute-start.18 = (f32[1280]{0:T(1024)S(1)}, f32[1280]{0:T(1024)S(1)}, u32[]{:S(2)}, u32[]{:S(2)}) collective-permute-start(f32[1280]{0:T(1024)S(1)} %collective-permute-done.15), channel_id=1, source_target_pairs={{0,1},{1,0},{2,3},{3,2},{4,5},{5,4},{6,7},{7,6},{8,9},{9,8},{10,11... | collective-permute-start | bytes 15368 | tf_op jit(solution)/shard_map/ppermute | solution.py:81
  314.4 29.9 %collective-permute-start.25 = (bf16[1024,1280]{1,0:T(8,128)(2,1)}, bf16[1024,1280]{1,0:T(8,128)(2,1)}, u32[]{:S(2)}, u32[]{:S(2)}) collective-permute-start(bf16[1024,1280]{1,0:T(8,128)(2,1)} %all-gather.13.cloned.1.call-done), channel_id=1, source_target_pairs={{0,1},{1,0},{2,3},{3,2},{4,5},{5,4},{6,7},{7,6},{8,9},{9,8},{10,11... | collective-permute-start | bytes 7864328 | tf_op jit(solution)/shard_map/ppermute | solution.py:81
  341.6 15.6 %collective-permute-start.21 = (bf16[1024,1024]{1,0:T(8,128)(2,1)S(1)}, bf16[1024,1024]{1,0:T(8,128)(2,1)}, u32[]{:S(2)}, u32[]{:S(2)}) collective-permute-start(bf16[1024,1024]{1,0:T(8,128)(2,1)S(1)} %convolution_convert_fusion.2.q_ref.own_ref), channel_id=1, source_target_pairs={{0,1},{1,0},{2,3},{3,2},{4,5},{5,4},{6,7},{7,6},{8,9},{9,8},{10,11... | collective-permute-start | bytes 6291464 | tf_op jit(solution)/shard_map/ppermute | solution.py:81
  341.8 77.6 %collective-permute-start.23 = (bf16[320,1280]{1,0:T(8,128)(2,1)S(1)}, bf16[320,1280]{1,0:T(8,128)(2,1)}, u32[]{:S(2)}, u32[]{:S(2)}) collective-permute-start(bf16[320,1280]{1,0:T(8,128)(2,1)S(1)} %bitcast.141), channel_id=1, source_target_pairs={{0,1},{1,0},{2,3},{3,2},{4,5},{5,4},{6,7},{7,6},{8,9},{9,8},{10,11... | collective-permute-start | bytes 2457608 | tf_op jit(solution)/shard_map/ppermute | solution.py:81
  342.2 56.0 %collective-permute-start.27 = (bf16[320,1280]{1,0:T(8,128)(2,1)S(1)}, bf16[320,1280]{1,0:T(8,128)(2,1)}, u32[]{:S(2)}, u32[]{:S(2)}) collective-permute-start(bf16[320,1280]{1,0:T(8,128)(2,1)S(1)} %bitcast.142), channel_id=1, source_target_pairs={{0,2},{2,0},{1,3},{3,1},{4,6},{6,4},{5,7},{7,5},{8,10},{10,8},{9,1... | collective-permute-start | bytes 2457608 | tf_op jit(solution)/shard_map/ppermute | solution.py:84
  343.3 60.3 %collective-permute-start.34 = (f32[1280]{0:T(1024)S(1)}, f32[1280]{0:T(1024)S(1)}, u32[]{:S(2)}, u32[]{:S(2)}) collective-permute-start(f32[1280]{0:T(1024)S(1)} %copy-done.33), channel_id=1, source_target_pairs={{0,2},{2,0},{1,3},{3,1},{4,6},{6,4},{5,7},{7,5},{8,10},{10,8},{9,1... | collective-permute-start | bytes 15368 | tf_op jit(solution)/shard_map/ppermute | solution.py:84
  349.9 24.2 %collective-permute-start.26 = (bf16[1024,1024]{1,0:T(8,128)(2,1)S(1)}, bf16[1024,1024]{1,0:T(8,128)(2,1)S(1)}, u32[]{:S(2)}, u32[]{:S(2)}) collective-permute-start(bf16[1024,1024]{1,0:T(8,128)(2,1)S(1)} %convolution_convert_fusion.q_ref.own_ref), channel_id=1, source_target_pairs={{0,1},{1,0},{2,3},{3,2},{4,5},{5,4},{6,7},{7,6},{8,9},{9,8},{10,11... | collective-permute-start | bytes 6291464 | tf_op jit(solution)/shard_map/ppermute | solution.py:81
  357.2 46.5 %collective-permute-start.22 = (bf16[1024,1024]{1,0:T(8,128)(2,1)S(1)}, bf16[1024,1024]{1,0:T(8,128)(2,1)S(1)}, u32[]{:S(2)}, u32[]{:S(2)}) collective-permute-start(bf16[1024,1024]{1,0:T(8,128)(2,1)S(1)} %convolution_convert_fusion.3.q_ref.own_ref), channel_id=1, source_target_pairs={{0,1},{1,0},{2,3},{3,2},{4,5},{5,4},{6,7},{7,6},{8,9},{9,8},{10,11... | collective-permute-start | bytes 6291464 | tf_op jit(solution)/shard_map/ppermute | solution.py:81
  375.4 49.2 %collective-permute-start.28 = (bf16[1024,1024]{1,0:T(8,128)(2,1)}, bf16[1024,1024]{1,0:T(8,128)(2,1)}, u32[]{:S(2)}, u32[]{:S(2)}) collective-permute-start(bf16[1024,1024]{1,0:T(8,128)(2,1)} %convolution_convert_fusion.1.q_ref.own_ref), channel_id=1, source_target_pairs={{0,1},{1,0},{2,3},{3,2},{4,5},{5,4},{6,7},{7,6},{8,9},{9,8},{10,11... | collective-permute-start | bytes 6291464 | tf_op jit(solution)/shard_map/ppermute | solution.py:81
  398.1 81.8 %collective-permute-start.30 = (bf16[1280,1280]{1,0:T(8,128)(2,1)}, bf16[1280,1280]{1,0:T(8,128)(2,1)}, u32[]{:S(2)}, u32[]{:S(2)}) collective-permute-start(bf16[1280,1280]{1,0:T(8,128)(2,1)} %get-tuple-element.21), channel_id=1, source_target_pairs={{0,1},{1,0},{2,3},{3,2},{4,5},{5,4},{6,7},{7,6},{8,9},{9,8},{10,11... | collective-permute-start | bytes 9830408 | tf_op jit(solution)/shard_map/ppermute | solution.py:81
  403.6 76.3 %collective-permute-start.32 = (bf16[1280,1280]{1,0:T(8,128)(2,1)}, bf16[1280,1280]{1,0:T(8,128)(2,1)}, u32[]{:S(2)}, u32[]{:S(2)}) collective-permute-start(bf16[1280,1280]{1,0:T(8,128)(2,1)} %get-tuple-element.25), channel_id=1, source_target_pairs={{0,1},{1,0},{2,3},{3,2},{4,5},{5,4},{6,7},{7,6},{8,9},{9,8},{10,11... | collective-permute-start | bytes 9830408 | tf_op jit(solution)/shard_map/ppermute | solution.py:81
  403.7 67.6 %collective-permute-start.37 = (f32[1280]{0:T(1024)S(1)}, f32[1280]{0:T(1024)S(1)}, u32[]{:S(2)}, u32[]{:S(2)}) collective-permute-start(f32[1280]{0:T(1024)S(1)} %collective-permute-done.34), channel_id=1, source_target_pairs={{0,1},{1,0},{2,3},{3,2},{4,5},{5,4},{6,7},{7,6},{8,9},{9,8},{10,11... | collective-permute-start | bytes 15368 | tf_op jit(solution)/shard_map/ppermute | solution.py:81
  419.4 22.2 %collective-permute-start.29 = (bf16[320,1280]{1,0:T(8,128)(2,1)}, bf16[320,1280]{1,0:T(8,128)(2,1)}, u32[]{:S(2)}, u32[]{:S(2)}) collective-permute-start(bf16[320,1280]{1,0:T(8,128)(2,1)} %collective-permute-done.27), channel_id=1, source_target_pairs={{0,1},{1,0},{2,3},{3,2},{4,5},{5,4},{6,7},{7,6},{8,9},{9,8},{10,11... | collective-permute-start | bytes 2457608 | tf_op jit(solution)/shard_map/ppermute | solution.py:81
  424.6 47.2 %collective-permute-start.36 = (bf16[1280,1280]{1,0:T(8,128)(2,1)}, bf16[1280,1280]{1,0:T(8,128)(2,1)}, u32[]{:S(2)}, u32[]{:S(2)}) collective-permute-start(bf16[1280,1280]{1,0:T(8,128)(2,1)} %all-gather.15.cloned.1.call-done), channel_id=1, source_target_pairs={{0,1},{1,0},{2,3},{3,2},{4,5},{5,4},{6,7},{7,6},{8,9},{9,8},{10,11... | collective-permute-start | bytes 9830408 | tf_op jit(solution)/shard_map/ppermute | solution.py:81
  441.7 30.1 %collective-permute-start.38 = (bf16[1280,1280]{1,0:T(8,128)(2,1)}, bf16[1280,1280]{1,0:T(8,128)(2,1)}, u32[]{:S(2)}, u32[]{:S(2)}) collective-permute-start(bf16[1280,1280]{1,0:T(8,128)(2,1)} %all-gather.17.cloned.1.call-done), channel_id=1, source_target_pairs={{0,1},{1,0},{2,3},{3,2},{4,5},{5,4},{6,7},{7,6},{8,9},{9,8},{10,11... | collective-permute-start | bytes 9830408 | tf_op jit(solution)/shard_map/ppermute | solution.py:81
  454.3 54.2 %copy-start.16 = (bf16[512,1280]{1,0:T(8,128)(2,1)}, bf16[512,1280]{1,0:T(8,128)(2,1)S(1)}, u32[]{:S(2)}) copy-start(bf16[512,1280]{1,0:T(8,128)(2,1)S(1)} %get-tuple-element.29) | copy-start | bytes 3932164
  471.3 8.6 %collective-permute-start.31 = (f32[1280]{0:T(1024)S(1)}, f32[1280]{0:T(1024)S(1)}, u32[]{:S(2)}, u32[]{:S(2)}) collective-permute-start(f32[1280]{0:T(1024)S(1)} %copy-done.33), channel_id=1, source_target_pairs={{0,1},{1,0},{2,3},{3,2},{4,5},{5,4},{6,7},{7,6},{8,9},{9,8},{10,11... | collective-permute-start | bytes 15368 | tf_op jit(solution)/shard_map/ppermute | solution.py:81
  490.7 30.7 %collective-permute-start.39 = (bf16[512,1280]{1,0:T(8,128)(2,1)}, bf16[512,1280]{1,0:T(8,128)(2,1)}, u32[]{:S(2)}, u32[]{:S(2)}) collective-permute-start(bf16[512,1280]{1,0:T(8,128)(2,1)} %fusion.47), channel_id=1, source_target_pairs={{0,2},{2,0},{1,3},{3,1},{4,6},{6,4},{5,7},{7,5},{8,10},{10,8},{9,1... | collective-permute-start | bytes 3932168 | tf_op jit(solution)/shard_map/ppermute | solution.py:84
  (34 other events, 138.1 us)
Sparse Core Ops, SparseCore 0:
  34.5 36.8 all-gather.6
  73.2 40.8 all-gather.8
  115.9 40.8 all-gather.10
  158.5 35.4 all-gather.12
  195.6 40.8 all-gather.14
  344.4 41.3 all-gather.16

commit v2 on v1

v2 whole, which is shorter than its diff:
```python
import functools
import math

import jax
import jax.numpy as jnp
from jax import lax
from jax.experimental import pallas as pl
from jax.experimental.pallas import tpu as pltpu
from jax.sharding import PartitionSpec as P

LN_EPS = 1e-5
LOG2E = math.log2(math.e)
SWAP_CORE = [(0, 1), (1, 0), (2, 3), (3, 2)]
SWAP_CHIP = [(0, 2), (2, 0), (1, 3), (3, 1)]


def layer_norm(rows, gain, shift):
    row_mean = jnp.mean(rows, axis=-1, keepdims=True)
    centred = rows - row_mean
    row_var = jnp.mean(centred * centred, axis=-1, keepdims=True)
    return (centred * lax.rsqrt(row_var + LN_EPS) * gain + shift).astype(jnp.bfloat16)


def attn_kernel(q_ref, own_ref, peer_ref, out_ref, vext_ref, *, scale):
    n = own_ref.shape[0]
    bq = q_ref.shape[0]

    @pl.when(pl.program_id(0) == 0)
    def _():
        vext_ref[:, :, 128:] = jnp.ones((3, 2 * n, 128), jnp.bfloat16)
        for i, col in enumerate((640, 768, 896)):
            vext_ref[i, :n, :128] = own_ref[:, col:col + 128]
            vext_ref[i, n:, :128] = peer_ref[:, col:col + 128]

    low = lax.broadcasted_iota(jnp.int32, (bq, 128), 1) < 64
    nt = (((1,), (1,)), ((), ()))
    outs = []
    for head in range(5):
        q = q_ref[:, head // 2 * 128:(head // 2 + 1) * 128]
        q = jnp.concatenate([q[:, 64:], q[:, :64]], axis=1)
        q = jnp.where(low, jnp.zeros_like(q), q) if head % 2 == 0 else jnp.where(low, q, jnp.zeros_like(q))
        kcol = (head + 5) // 2 * 128
        pair = head // 2
        s_own = lax.dot_general(q, own_ref[:, kcol:kcol + 128], nt, preferred_element_type=jnp.float32)
        s_peer = lax.dot_general(q, peer_ref[:, kcol:kcol + 128], nt, preferred_element_type=jnp.float32)
        top = jnp.maximum(jnp.max(s_own, axis=1, keepdims=True), jnp.max(s_peer, axis=1, keepdims=True))
        p_own = jnp.exp2((s_own - top) * scale).astype(jnp.bfloat16)
        p_peer = jnp.exp2((s_peer - top) * scale).astype(jnp.bfloat16)
        o = jnp.dot(p_own, vext_ref[pair, :n, :], preferred_element_type=jnp.float32)
        o = o + jnp.dot(p_peer, vext_ref[pair, n:, :], preferred_element_type=jnp.float32)
        outs.append(o[:, :128] / o[:, 128:])
    out_ref[:, 0:128] = jnp.where(low, outs[0], outs[1]).astype(jnp.bfloat16)
    out_ref[:, 128:256] = jnp.where(low, outs[2], outs[3]).astype(jnp.bfloat16)
    out_ref[:, 256:320] = outs[4][:, :64].astype(jnp.bfloat16)


def whole(a):
    return pl.BlockSpec(a.shape, lambda i: (0,) * a.ndim)


def row_block(block, width):
    return pl.BlockSpec((block, width), lambda i: (i, 0))


def of_layer(w, layer):
    index = layer if w.shape[0] > 1 else 0
    return pl.BlockSpec((1,) + w.shape[1:], lambda i: (index, 0, 0))


def qkv_kernel(h_ref, w0_ref, w1_ref, out0_ref, out1_ref):
    f = w0_ref.shape[1]
    for w, out in ((w0_ref, out0_ref), (w1_ref, out1_ref)):
        out[:, f:] = jnp.zeros((out.shape[0], out.shape[1] - f), jnp.bfloat16)
        out[:, :f] = lax.dot_general(h_ref[...], w[0], (((1,), (1,)), ((), ())), preferred_element_type=jnp.float32).astype(jnp.bfloat16)


def project(h, w0, w1, layer, block=256):
    n, d = h.shape
    f = w0.shape[1]
    return pl.pallas_call(
        qkv_kernel,
        grid=(n // block,),
        in_specs=[row_block(block, d), of_layer(w0, layer), of_layer(w1, layer)],
        out_specs=(row_block(block, 1024),) * 2,
        out_shape=(jax.ShapeDtypeStruct((n, 1024), jnp.bfloat16),) * 2,
        compiler_params=pltpu.CompilerParams(vmem_limit_bytes=40 * 2 ** 20),
        cost_estimate=pl.CostEstimate(flops=4 * n * d * f, bytes_accessed=2 * n * d + 4 * f * d + 4 * n * f, transcendentals=0),
    )(h, w0, w1)


def out_kernel(r_ref, bias_ref, norm_ref, a0, a1, a2, a3, w0, w1, w2, w3, r_out, h_out):
    acc = r_ref[...] + bias_ref[...]
    for a, w in ((a0, w0), (a1, w1), (a2, w2), (a3, w3)):
        acc = acc + jnp.dot(a[...], w[0], preferred_element_type=jnp.float32)
    r_out[...] = acc
    h_out[...] = layer_norm(acc, norm_ref[0:1, :], norm_ref[1:2, :])


def out_proj(r, bias, norm, attns, ws, layer, block=256):
    n, d = r.shape
    f = attns[0].shape[1]
    return pl.pallas_call(
        out_kernel,
        grid=(n // block,),
        in_specs=[row_block(block, d), whole(bias), whole(norm)] + [row_block(block, f)] * 4 + [of_layer(w, layer) for w in ws],
        out_specs=(row_block(block, d),) * 2,
        out_shape=(jax.ShapeDtypeStruct((n, d), jnp.float32), jax.ShapeDtypeStruct((n, d), jnp.bfloat16)),
        compiler_params=pltpu.CompilerParams(vmem_limit_bytes=40 * 2 ** 20),
        cost_estimate=pl.CostEstimate(flops=8 * n * d * f, bytes_accessed=12 * n * d + 8 * f * d, transcendentals=0),
    )(r, bias, norm, *attns, *ws)


def mlp_kernel(h_ref, r_ref, bdown_ref, bias_ref, norm_ref, *refs, pick, normed):
    count = len(pick)
    ws, refs = refs[:2 * count], refs[2 * count:]
    out_ref, hn_ref = refs[0], refs[1] if normed else None
    up_ref, down_ref, u_ref, acc_ref, sems = refs[1 + normed:]
    first = pl.program_id(0) == 0
    d, f = h_ref.shape[1], u_ref.shape[1]
    chunk = 256

    def copies(s):
        for which, dst in ((0, up_ref), (1, down_ref)):
            yield pltpu.make_async_copy(ws[2 * s + which].at[pick[s][which]], dst.at[s], sems.at[s, which])

    @pl.when(first)
    def _():
        for s in range(count):
            for copy in copies(s):
                copy.start()

    acc_ref[...] = r_ref[...] + bdown_ref[...]
    for s in range(count):
        @pl.when(first)
        def _():
            for copy in copies(s):
                copy.wait()

        for n in range(f // chunk):
            cols = slice(n * chunk, (n + 1) * chunk)
            u = jnp.dot(h_ref[...], up_ref[s, :, :, cols].reshape(d, chunk), preferred_element_type=jnp.float32) + bias_ref[s:s + 1, cols]
            u_ref[:, cols] = jax.nn.gelu(u, approximate=True).astype(jnp.bfloat16)
        for n in range(d // chunk):
            cols = slice(n * chunk, (n + 1) * chunk)
            acc_ref[:, cols] += jnp.dot(u_ref[...], down_ref[s, :, :, cols].reshape(f, chunk), preferred_element_type=jnp.float32)
    out_ref[...] = acc_ref[...].astype(out_ref.dtype)
    if normed:
        hn_ref[...] = layer_norm(acc_ref[...], norm_ref[0:1, :], norm_ref[1:2, :])


def mlp(h, r, bdown, norm, shards, normed=False, dtype=jnp.float32, part=None, block=512):
    d = h.shape[1]
    start, n = part or (0, h.shape[0])
    offset = start // block
    count = len(shards)
    pick = [s[2] for s in shards]
    weights = [w for s in shards for w in s[1]]
    bias = jnp.stack([s[0] for s in shards])
    f = bias.shape[1]
    rows_in = pl.BlockSpec((block, d), lambda i: (i + offset, 0))
    out_shape = [jax.ShapeDtypeStruct((n, d), dtype)]
    if normed:
        out_shape.append(jax.ShapeDtypeStruct((n, d), jnp.bfloat16))
    return pl.pallas_call(
        functools.partial(mlp_kernel, pick=pick, normed=normed),
        grid=(n // block,),
        in_specs=[rows_in, rows_in, whole(bdown), whole(bias), whole(norm)] + [pl.BlockSpec(memory_space=pl.ANY)] * (2 * count),
        out_specs=[row_block(block, d)] * len(out_shape),
        out_shape=out_shape,
        scratch_shapes=[
            pltpu.VMEM((count, 4, d // 4, f), jnp.bfloat16),
            pltpu.VMEM((count, 4, f // 4, d), jnp.bfloat16),
            pltpu.VMEM((block, f), jnp.bfloat16),
            pltpu.VMEM((block, d), jnp.float32),
            pltpu.SemaphoreType.DMA((count, 2)),
        ],
        compiler_params=pltpu.CompilerParams(vmem_limit_bytes=60 * 2 ** 20),
        cost_estimate=pl.CostEstimate(flops=count * 4 * n * d * f, bytes_accessed=count * 4 * d * f + 8 * n * d, transcendentals=count * n * f),
    )(h, r, bdown, bias, norm, *weights)


def attention(own, peer, block=512):
    n = own.shape[0]
    return pl.pallas_call(
        functools.partial(attn_kernel, scale=64 ** -0.5 * LOG2E),
        grid=(n // block,),
        in_specs=[
            row_block(block, 1024),
            whole(own),
            whole(own),
        ],
        out_specs=row_block(block, 320),
        out_shape=jax.ShapeDtypeStruct((n, 320), jnp.bfloat16),
        scratch_shapes=[pltpu.VMEM((3, 2 * n, 256), jnp.bfloat16)],
        compiler_params=pltpu.CompilerParams(vmem_limit_bytes=48 * 2 ** 20),
        cost_estimate=pl.CostEstimate(flops=5 * 4 * n * 2 * n * 256, bytes_accessed=6 * 2 ** 20, transcendentals=10 * n * n),
    )(own, own, peer)


def solution(mesh):
    def swap_core(a):
        return lax.ppermute(a, 'tp', SWAP_CORE)

    def swap_chip(a):
        return lax.ppermute(a, 'tp', SWAP_CHIP)

    def after(a, *earlier):
        return lax.optimization_barrier((a, *earlier))[0]

    def local_layers(hidden_in, norms, w_qkv, w_out, b_out, w_up, b_up, w_down, b_down):
        n_layers, model = w_qkv.shape[:2]
        hidden = w_up.shape[2]
        chip = lax.axis_index('tp') // 2
        group = lax.axis_index('dp')
        n_groups = mesh.shape['dp']

        def piece(a, l):
            rows = a.shape[1] // n_groups
            return lax.dynamic_slice(a, (l, group * rows, 0), (1, rows, a.shape[2]))

        def gathered(a):
            return lax.all_gather(a, 'dp', axis=0, tiled=True)

        sent = lax.dynamic_index_in_dim(hidden_in, 1 - chip, 0, keepdims=False)
        visiting = swap_chip(sent)
        kept = lax.dynamic_index_in_dim(hidden_in, chip, 0, keepdims=False)
        block = kept.shape[0]

        wt = jnp.transpose(w_qkv, (0, 2, 3, 4, 1)).reshape(n_layers, -1, model)
        wo = w_out.reshape(n_layers, -1, model)
        up4 = w_up.reshape(n_layers, 4, model // 4, hidden)
        down4 = w_down.reshape(n_layers, 4, hidden // 4, model)

        def fetch_qkv(l, *earlier):
            return gathered(swap_chip(after(piece(wt, l)[0], *earlier)))[None]

        def fetch_mlp(l, *earlier):
            both = jnp.concatenate([piece(w_up, l), piece(w_down, l)], axis=0)
            return gathered(swap_chip(after(both, *earlier))[None])

        wt_partner = swap_core(after(wt, sent))
        qkv_far = fetch_qkv(0, sent)
        mlp_far = fetch_mlp(0, visiting)
        residual = jnp.concatenate([kept, visiting], axis=0).astype(jnp.float32)
        normed = layer_norm(residual, norms[0, 0], norms[0, 1])

        for l in range(n_layers):
            own, partner = project(normed, wt, wt_partner, l)
            if l == 0:
                wo_partner, up_partner, down_partner, bup_partner = (swap_core(after(a, own)) for a in (wo, up4, down4, b_up))
                bup_far = swap_chip(after(b_up, own))
                bup_diag = swap_core(bup_far)
            attn0 = attention(own, swap_core(partner))
            attn1 = attention(after(partner, attn0), swap_core(own))
            qkv_far = after(qkv_far, attn0)
            out_far = swap_chip(after(wo[l:l + 1], attn0))
            out_diag = swap_core(out_far)
            far, diag = project(after(normed, attn1), qkv_far, swap_core(qkv_far), l)
            attn2 = attention(far, swap_core(diag))
            attn3 = attention(after(diag, attn2), swap_core(far))
            if l + 1 < n_layers:
                qkv_far = fetch_qkv(l + 1, attn3)
            residual, normed2 = out_proj(residual, b_out[l:l + 1], norms[l, 2:4], (attn0, attn1, attn2, attn3), (wo, wo_partner, out_far, out_diag), l)

            mlp_diag = swap_core(mlp_far)
            near = [(b_up[l], (up4, down4), (l, l)), (bup_partner[l], (up_partner, down_partner), (l, l))]
            every = slice(None)
            far_sh = (bup_far[l], (mlp_far, mlp_far), ((every, 0), (every, 1)))
            diag_sh = (bup_diag[l], (mlp_diag, mlp_diag), ((every, 0), (every, 1)))
            bd = b_down[l:l + 1]
            if l + 1 < n_layers:
                norm = norms[l + 1, 0:2]
                residual, = mlp(normed2, residual, bd, norm, near)
                residual, = mlp(normed2, residual, jnp.zeros_like(bd), norm, [far_sh])
                mlp_far = fetch_mlp(l + 1, residual)
                residual, normed = mlp(normed2, residual, jnp.zeros_like(bd), norm, [diag_sh], normed=True)
            else:
                shards = near + [far_sh, diag_sh]
                last, = mlp(normed2, residual, bd, norms[l, 0:2], shards, dtype=jnp.bfloat16, part=(block, block))
                back = swap_chip(last)
                stay, = mlp(after(normed2, last), residual, bd, norms[l, 0:2], shards, dtype=jnp.bfloat16, part=(0, block))
        first = chip == 0
        return jnp.stack([jnp.where(first, stay, back), jnp.where(first, back, stay)])

    in_specs = (P('dp', 'tp', None), P(), P(None, None, None, 'tp', None), P(None, 'tp', None, None), P(), P(None, None, 'tp'), P(None, 'tp'), P(None, 'tp', None), P())
    return jax.shard_map(local_layers, mesh=mesh, in_specs=in_specs, out_specs=P('dp', 'tp', None), check_vma=False)
```

time: 548 us -> 532 us (0.971)
  matrix products: 212 us -> 0 us
  Pallas kernels: 129 us -> 288 us
  waiting for transfers between devices: 104 us -> 159 us
  local copies, waits for them, and re-layouts: 47.4 us -> 38.8 us
  starting transfers between devices: 22.4 us -> 15.7 us
    dot_general x28 -> x0, matrix products: 212 us -> none  [the longest x12 125 us: mlp(): acc = acc + jnp.dot(u, down_sh[s], preferred_element_type=jnp.float32)]
    pallas_call x0 -> x11, Pallas kernels: none -> 151 us  [the longest x5 97.4 us: mlp(): pl.pallas_call(functools.partial(mlp_kernel, pick=pick, normed=normed), g...]
    ppermute x12 -> x9, waiting for transfers between devices: 104 us -> 138 us  [swap_chip(): return lax.ppermute(a, 'tp', SWAP_CHIP)]
    all_gather x6 -> x4, waiting for transfers between devices: 0.05 us -> 17.5 us  [gathered(): return lax.all_gather(a, 'dp', axis=0, tiled=True)]
    squeeze x2, local copies, waits for them, and re-layouts: 11.7 us -> 2.75 us  [the longest x1 2.16 us: fetch_qkv(): return gathered(swap_chip(after(piece(wt, l)[0], *earlier)))[None]]
    unnamed x79 -> x84, local copies, waits for them, and re-layouts: 18.2 us -> 26.4 us
    pallas_call x8, Pallas kernels: 129 us -> 137 us  [attention(): pl.pallas_call(functools.partial(attn_kernel, scale=64 ** (-0.5) * LOG2E)...]
    ppermute x12 -> x9, starting transfers between devices: 15.6 us -> 11.1 us  [swap_chip(): return lax.ppermute(a, 'tp', SWAP_CHIP)]
  transfers between devices with their start and end apart: 46 -> 33, of which waited for: 7 -> 12; matrix products, arithmetic and copies ran while one was open for 42% -> 3% of each run, Pallas kernels for 24% -> 50%
where the time goes in v2:
time: 532 us; the launch traced here: 528 us
  Pallas kernels  288 us (54%)
  waiting for transfers between devices  159 us (30%)
  local copies, waits for them, and re-layouts  38.8 us (7%)
  starting transfers between devices  15.7 us (3%)
  between operations  14.1 us (3%)
  other arithmetic  11.8 us (2%)
    ppermute x9, waiting for transfers between devices, swap_chip(): return lax.ppermute(a, 'tp', SWAP_CHIP)  138 us
    pallas_call x8, Pallas kernels, attention(): pl.pallas_call(functools.partial(attn_kernel, scale=64 ** (-0.5) * LOG2E)...  137 us
    pallas_call x5, Pallas kernels, mlp(): pl.pallas_call(functools.partial(mlp_kernel, pick=pick, normed=normed), g...  97.4 us
    pallas_call x4, Pallas kernels, project(): pl.pallas_call(qkv_kernel, grid=(n // block,), in_specs=[row_block(block,...  33.3 us
    unnamed x84, local copies, waits for them, and re-layouts  26.4 us
    pallas_call x2, Pallas kernels, out_proj(): pl.pallas_call(out_kernel, grid=(n // block,), in_specs=[row_block(block,...  20.5 us
    all_gather x4, waiting for transfers between devices, gathered(): return lax.all_gather(a, 'dp', axis=0, tiled=True)  17.5 us
    ppermute x9, starting transfers between devices, swap_chip(): return lax.ppermute(a, 'tp', SWAP_CHIP)  11.1 us
  transfers between devices with their start and end apart: 33, of which 12 were waited for; matrix products, arithmetic and copies ran while one was open for 3% of the time, Pallas kernels for 50%

profile of v2, /device:TPU:0, one launch (start us, length us, event | category | flops | bytes accessed | tf_op | source)
XLA Modules:
  0.0 528.0 jit_solution(15633004103273065142)
XLA Ops:
  6.5 2.9 dynamic-slice_bitcast_fusion.1
  10.2 2.2 dynamic-slice_bitcast_fusion.2
  12.4 3.0 collective-permute-start.4
  15.4 14.7 %collective-permute-done.4 = bf16[240,1280]{1,0:T(8,128)(2,1)S(1)} collective-permute-done((bf16[240,1280]{1,0:T(8,128)(2,1)S(1)}, bf16[240,1280]{1,0:T(8,128)(2,1)S(1)}, u32[]{:S(2)}, u32[]{:S(2)}) %collective-permute-start.4) | collective-permute-done | bytes 614432 | tf_op jit(solution)/shard_map/ppermute | solution.py:205
  31.0 3.3 constant_dynamic-slice_fusion
  34.5 23.0 %collective-permute-done = bf16[512,1280]{1,0:T(8,128)(2,1)S(1)} collective-permute-done((bf16[512,1280]{1,0:T(8,128)(2,1)}, bf16[512,1280]{1,0:T(8,128)(2,1)S(1)}, u32[]{:S(2)}, u32[]{:S(2)}) %collective-permute-start) | collective-permute-done | bytes 1310752 | tf_op jit(solution)/shard_map/ppermute | solution.py:205
  57.5 1.7 collective-permute-start.15
  60.5 2.0 add_convert_fusion.h_ref
  62.6 9.7 %shard_map.91 = (bf16[1024,1024]{1,0:T(8,128)(2,1)S(1)}, bf16[1024,1024]{1,0:T(8,128)(2,1)S(1)}) custom-call(bf16[1024,1280]{1,0:T(8,128)(2,1)S(1)} %add_convert_fusion.h_ref, bf16[2,960,1280]{2,1,0:T(8,128)(2,1)} %bitcast.4.w0_ref, bf16[2,960,1280]{2,1,0:T(8,128)(2,1)} %collective-permute-done.1.w1_ref), custom_call_target="tpu_custom_call" | custom-call | flops 5033164800 | bytes 11468800 | tf_op jit(solution)/shard_map/pallas_call | solution.py:80
  73.6 21.1 %collective-permute-done.15 = bf16[2,320,1280]{2,1,0:T(8,128)(2,1)} collective-permute-done((bf16[2,320,1280]{2,1,0:T(8,128)(2,1)S(1)}, bf16[2,320,1280]{2,1,0:T(8,128)(2,1)}, u32[]{:S(2)}, u32[]{:S(2)}) %collective-permute-start.15) | collective-permute-done | bytes 1638432 | tf_op jit(solution)/shard_map/ppermute | solution.py:205
  95.2 1.6 copy-done.22
  96.8 16.9 %shard_map.92.a0 = bf16[1024,320]{1,0:T(8,128)(2,1)S(1)} custom-call(bf16[1024,1024]{1,0:T(8,128)(2,1)S(1)} %copy-done.22, bf16[1024,1024]{1,0:T(8,128)(2,1)S(1)} %copy-done.22, bf16[1024,1024]{1,0:T(8,128)(2,1)} %collective-permute-done.2.peer_ref), custom_call_target="tpu_custom_call" | custom-call | flops 10737418240 | bytes 6291456 | tf_op jit(solution)/shard_map/pallas_call | solution.py:184
  116.2 1.8 copy-done.20
  118.1 17.4 %shard_map.93.a1 = bf16[1024,320]{1,0:T(8,128)(2,1)S(1)} custom-call(bf16[1024,1024]{1,0:T(8,128)(2,1)S(1)} %copy-done.20, bf16[1024,1024]{1,0:T(8,128)(2,1)S(1)} %copy-done.20, bf16[1024,1024]{1,0:T(8,128)(2,1)} %collective-permute-done.3.peer_ref), custom_call_target="tpu_custom_call" | custom-call | flops 10737418240 | bytes 6291456 | tf_op jit(solution)/shard_map/pallas_call | solution.py:184
  135.5 6.4 %shard_map.94 = (bf16[1024,1024]{1,0:T(8,128)(2,1)}, bf16[1024,1024]{1,0:T(8,128)(2,1)S(1)}) custom-call(bf16[1024,1280]{1,0:T(8,128)(2,1)S(1)} %copy-done.4, bf16[1,960,1280]{2,1,0:T(8,128)(2,1)S(1)} %bitcast.36, bf16[1,960,1280]{2,1,0:T(8,128)(2,1)S(1)} %collective-permute-done.5.w1_ref), custom_call_target="tpu_custom_call" | custom-call | flops 5033164800 | bytes 11468800 | tf_op jit(solution)/shard_map/pallas_call | solution.py:80
  145.7 2.7 fusion.r_ref
  149.2 1.5 collective-permute-start.14
  151.3 17.6 %shard_map.95.a2 = bf16[1024,320]{1,0:T(8,128)(2,1)S(1)} custom-call(bf16[1024,1024]{1,0:T(8,128)(2,1)} %get-tuple-element.46.q_ref.own_ref, bf16[1024,1024]{1,0:T(8,128)(2,1)} %get-tuple-element.46.q_ref.own_ref, bf16[1024,1024]{1,0:T(8,128)(2,1)S(1)} %collective-permute-done.6.peer_ref), custom_call_target="tpu_custom_call" | custom-call | flops 10737418240 | bytes 6291456 | tf_op jit(solution)/shard_map/pallas_call | solution.py:184
  171.2 15.5 %shard_map.96.a3 = bf16[1024,320]{1,0:T(8,128)(2,1)S(1)} custom-call(bf16[1024,1024]{1,0:T(8,128)(2,1)S(1)} %copy-done.18, bf16[1024,1024]{1,0:T(8,128)(2,1)S(1)} %copy-done.18, bf16[1024,1024]{1,0:T(8,128)(2,1)S(1)} %collective-permute-done.7.peer_ref), custom_call_target="tpu_custom_call" | custom-call | flops 10737418240 | bytes 6291456 | tf_op jit(solution)/shard_map/pallas_call | solution.py:184
  189.5 13.9 %collective-permute-done.20 = bf16[240,1280]{1,0:T(8,128)(2,1)} collective-permute-done((bf16[240,1280]{1,0:T(8,128)(2,1)S(1)}, bf16[240,1280]{1,0:T(8,128)(2,1)}, u32[]{:S(2)}, u32[]{:S(2)}) %collective-permute-start.20) | collective-permute-done | bytes 614432 | tf_op jit(solution)/shard_map/ppermute | solution.py:205
  208.1 10.5 %shard_map.97 = (f32[1024,1280]{1,0:T(8,128)}, bf16[1024,1280]{1,0:T(8,128)(2,1)S(1)}) custom-call(f32[1024,1280]{1,0:T(8,128)} %fusion.r_ref, f32[1,1280]{1,0:T(1,128)S(1)} %get-tuple-element.101.bias_ref, f32[2,1280]{1,0:T(2,128)S(1)} %get-tuple-element.88.norm_ref, bf16[1024,320]{1,0:T(8,128)(2,1)S(1)} %copy-done.6, bf16[1024,320]{1,0:T(8,128)(2,1)S(1)} %copy-done.8, ...), custom_call_target="tpu_custom_call" | custom-call | flops 3355443200 | bytes 19005440 | tf_op jit(solution)/shard_map/pallas_call | solution.py:102
  218.6 1.5 copy-done.2
  220.1 23.4 %shard_map.98.r_ref = f32[1024,1280]{1,0:T(8,128)} custom-call(bf16[1024,1280]{1,0:T(8,128)(2,1)} %copy-done.2, f32[1024,1280]{1,0:T(8,128)} %get-tuple-element.52.r_ref, f32[1,1280]{1,0:T(1,128)} %get-tuple-element.99.bdown_ref, f32[2,1280]{1,0:T(2,128)} %pad_maximum_fusion.5.bias_ref, f32[2,1280]{1,0:T(2,128)} %get-tuple-element.89.norm_ref, ...), custom_call_target="tpu_custom_call" | custom-call | flops 13421772800 | bytes 23592960 | tf_op jit(solution)/shard_map/pallas_call | solution.py:164
  244.1 14.7 %shard_map.99.r_ref = f32[1024,1280]{1,0:T(8,128)} custom-call(bf16[1024,1280]{1,0:T(8,128)(2,1)} %copy-done.2, f32[1024,1280]{1,0:T(8,128)} %shard_map.98.r_ref, f32[1,1280]{1,0:T(1,128)} %broadcast_2_bdown_ref.2.bdown_ref, f32[1,1280]{1,0:T(1,128)} %get-tuple-element.95.bias_ref, f32[2,1280]{1,0:T(2,128)} %get-tuple-element.89.norm_ref, ...), custom_call_target="tpu_custom_call" | custom-call | flops 6710886400 | bytes 17039360 | tf_op jit(solution)/shard_map/pallas_call | solution.py:164
  259.5 37.5 %collective-permute-done.26 = bf16[2,320,1280]{2,1,0:T(8,128)(2,1)} collective-permute-done((bf16[2,320,1280]{2,1,0:T(8,128)(2,1)}, bf16[2,320,1280]{2,1,0:T(8,128)(2,1)}, u32[]{:S(2)}, u32[]{:S(2)}) %collective-permute-start.26) | collective-permute-done | bytes 1638432 | tf_op jit(solution)/shard_map/ppermute | solution.py:205
  298.9 16.2 %shard_map.100 = (f32[1024,1280]{1,0:T(8,128)}, bf16[1024,1280]{1,0:T(8,128)(2,1)}) custom-call(bf16[1024,1280]{1,0:T(8,128)(2,1)} %copy-done.2, f32[1024,1280]{1,0:T(8,128)} %shard_map.99.r_ref, f32[1,1280]{1,0:T(1,128)} %broadcast_2_bdown_ref.2.bdown_ref, f32[1,1280]{1,0:T(1,128)} %get-tuple-element.97.bias_ref, f32[2,1280]{1,0:T(2,128)} %get-tuple-element.89.norm_ref, ...), custom_call_target="tpu_custom_call" | custom-call | flops 6710886400 | bytes 17039360 | tf_op jit(solution)/shard_map/pallas_call | solution.py:164
  315.1 1.7 copy-done.27
  316.8 8.9 %shard_map.101 = (bf16[1024,1024]{1,0:T(8,128)(2,1)}, bf16[1024,1024]{1,0:T(8,128)(2,1)S(1)}) custom-call(bf16[1024,1280]{1,0:T(8,128)(2,1)S(1)} %copy-done.27, bf16[2,960,1280]{2,1,0:T(8,128)(2,1)} %bitcast.4.w0_ref, bf16[2,960,1280]{2,1,0:T(8,128)(2,1)} %collective-permute-done.1.w1_ref), custom_call_target="tpu_custom_call" | custom-call | flops 5033164800 | bytes 11468800 | tf_op jit(solution)/shard_map/pallas_call | solution.py:80
  327.5 2.3 collective-permute-done.18.peer_ref
  329.9 17.4 %shard_map.102.a0 = bf16[1024,320]{1,0:T(8,128)(2,1)S(1)} custom-call(bf16[1024,1024]{1,0:T(8,128)(2,1)} %get-tuple-element.59.q_ref.own_ref, bf16[1024,1024]{1,0:T(8,128)(2,1)} %get-tuple-element.59.q_ref.own_ref, bf16[1024,1024]{1,0:T(8,128)(2,1)S(1)} %collective-permute-done.18.peer_ref), custom_call_target="tpu_custom_call" | custom-call | flops 10737418240 | bytes 6291456 | tf_op jit(solution)/shard_map/pallas_call | solution.py:184
  348.4 17.5 %all-gather.13.cloned.1.call-done = bf16[8,320,1280]{2,1,0:T(8,128)(2,1)} async-done(((bf16[2,320,1280]{2,1,0:T(8,128)(2,1)}), bf16[8,320,1280]{2,1,0:T(8,128)(2,1)}) %all-gather.13.cloned.1.call-update) | async-done | bytes 6553616 | tf_op jit(solution)/shard_map/all_gather | solution.py:222
  365.8 1.7 copy-done.24
  367.6 17.1 %shard_map.103.a1 = bf16[1024,320]{1,0:T(8,128)(2,1)S(1)} custom-call(bf16[1024,1024]{1,0:T(8,128)(2,1)S(1)} %copy-done.24, bf16[1024,1024]{1,0:T(8,128)(2,1)S(1)} %copy-done.24, bf16[1024,1024]{1,0:T(8,128)(2,1)} %collective-permute-done.19.peer_ref), custom_call_target="tpu_custom_call" | custom-call | flops 10737418240 | bytes 6291456 | tf_op jit(solution)/shard_map/pallas_call | solution.py:184
  384.7 1.7 copy-done.28
  386.4 8.2 %shard_map.104 = (bf16[1024,1024]{1,0:T(8,128)(2,1)}, bf16[1024,1024]{1,0:T(8,128)(2,1)S(1)}) custom-call(bf16[1024,1280]{1,0:T(8,128)(2,1)S(1)} %copy-done.28, bf16[1,960,1280]{2,1,0:T(8,128)(2,1)S(1)} %bitcast.34, bf16[1,960,1280]{2,1,0:T(8,128)(2,1)} %collective-permute-done.21.w1_ref), custom_call_target="tpu_custom_call" | custom-call | flops 5033164800 | bytes 11468800 | tf_op jit(solution)/shard_map/pallas_call | solution.py:80
  395.1 1.5 collective-permute-start.24
  397.2 18.4 %collective-permute-done.24.w2 = bf16[1,320,1280]{2,1,0:T(8,128)(2,1)S(1)} collective-permute-done((bf16[1,320,1280]{2,1,0:T(8,128)(2,1)S(1)}, bf16[1,320,1280]{2,1,0:T(8,128)(2,1)S(1)}, u32[]{:S(2)}, u32[]{:S(2)}) %collective-permute-start.24) | collective-permute-done | bytes 819232 | tf_op jit(solution)/shard_map/ppermute | solution.py:205
  417.0 1.6 copy-done.26
  418.6 17.8 %shard_map.105.a2 = bf16[1024,320]{1,0:T(8,128)(2,1)S(1)} custom-call(bf16[1024,1024]{1,0:T(8,128)(2,1)} %get-tuple-element.65.q_ref.own_ref, bf16[1024,1024]{1,0:T(8,128)(2,1)} %get-tuple-element.65.q_ref.own_ref, bf16[1024,1024]{1,0:T(8,128)(2,1)S(1)} %copy-done.26), custom_call_target="tpu_custom_call" | custom-call | flops 10737418240 | bytes 6291456 | tf_op jit(solution)/shard_map/pallas_call | solution.py:184
  436.4 17.1 %shard_map.106.a3 = bf16[1024,320]{1,0:T(8,128)(2,1)S(1)} custom-call(bf16[1024,1024]{1,0:T(8,128)(2,1)S(1)} %get-tuple-element.67.q_ref.own_ref, bf16[1024,1024]{1,0:T(8,128)(2,1)S(1)} %get-tuple-element.67.q_ref.own_ref, bf16[1024,1024]{1,0:T(8,128)(2,1)} %collective-permute-done.23.peer_ref), custom_call_target="tpu_custom_call" | custom-call | flops 10737418240 | bytes 6291456 | tf_op jit(solution)/shard_map/pallas_call | solution.py:184
  453.5 10.0 %shard_map.107 = (f32[1024,1280]{1,0:T(8,128)}, bf16[1024,1280]{1,0:T(8,128)(2,1)S(1)}) custom-call(f32[1024,1280]{1,0:T(8,128)} %get-tuple-element.57.r_ref, f32[1,1280]{1,0:T(1,128)S(1)} %get-tuple-element.100.bias_ref, f32[2,1280]{1,0:T(2,128)S(1)} %get-tuple-element.87.norm_ref, bf16[1024,320]{1,0:T(8,128)(2,1)S(1)} %copy-done.10, ...), custom_call_target="tpu_custom_call" | custom-call | flops 3355443200 | bytes 19005440 | tf_op jit(solution)/shard_map/pallas_call | solution.py:102
  463.6 1.5 copy-done.1
  465.1 21.5 %shard_map.108 = bf16[512,1280]{1,0:T(8,128)(2,1)} custom-call(bf16[1024,1280]{1,0:T(8,128)(2,1)} %copy-done.1, f32[1024,1280]{1,0:T(8,128)} %get-tuple-element.70.r_ref, f32[1,1280]{1,0:T(1,128)} %get-tuple-element.98.bdown_ref, f32[4,1280]{1,0:T(4,128)} %pad_maximum_fusion.4.bias_ref, f32[2,1280]{1,0:T(2,128)} %get-tuple-element.89.norm_ref, ...), custom_call_target="tpu_custom_call" | custom-call | flops 13421772800 | bytes 31457280 | tf_op jit(solution)/shard_map/pallas_call | solution.py:164
  486.5 1.5 collective-permute-start.28
  488.1 21.7 %shard_map.109 = bf16[512,1280]{1,0:T(8,128)(2,1)} custom-call(bf16[1024,1280]{1,0:T(8,128)(2,1)} %copy-done.1, f32[1024,1280]{1,0:T(8,128)} %get-tuple-element.70.r_ref, f32[1,1280]{1,0:T(1,128)} %get-tuple-element.98.bdown_ref, f32[4,1280]{1,0:T(4,128)} %pad_maximum_fusion.4.bias_ref, f32[2,1280]{1,0:T(2,128)} %get-tuple-element.89.norm_ref, ...), custom_call_target="tpu_custom_call" | custom-call | flops 13421772800 | bytes 31457280 | tf_op jit(solution)/shard_map/pallas_call | solution.py:164
  509.8 8.0 %collective-permute-done.28 = bf16[512,1280]{1,0:T(8,128)(2,1)S(1)} collective-permute-done((bf16[512,1280]{1,0:T(8,128)(2,1)}, bf16[512,1280]{1,0:T(8,128)(2,1)S(1)}, u32[]{:S(2)}, u32[]{:S(2)}) %collective-permute-start.28) | collective-permute-done | bytes 1310752 | tf_op jit(solution)/shard_map/ppermute | solution.py:205
  517.8 1.5 select_bitcast_fusion.1
  519.3 1.7 pad_maximum_fusion.1
  (150 shorter events, 30.7 us)
Async XLA Ops:
  6.5 108.0 %all-gather.7.cloned.1.call-start = ((), (), s32[]{:S(2)}) async-start(), calls=%async_computation | async-start | bytes 3072000 | tf_op jit(solution)/shard_map/all_gather | solution.py:222
  9.5 51.0 %copy-start.29 = (bf16[512,1280]{1,0:T(8,128)(2,1)}, bf16[512,1280]{1,0:T(8,128)(2,1)S(1)}, u32[]{:S(2)}) copy-start(bf16[512,1280]{1,0:T(8,128)(2,1)S(1)} %get-tuple-element.83) | copy-start | bytes 3932164
  9.5 21.5 %copy-start.38 = (f32[2,4,1280]{2,1,0:T(4,128)S(1)}, f32[2,4,1280]{2,1,0:T(4,128)}, u32[]{:S(2)}) copy-start(f32[2,4,1280]{2,1,0:T(4,128)} %param.10) | copy-start | bytes 122884
  9.5 53.1 %collective-permute-start.1 = (bf16[2,960,1280]{2,1,0:T(8,128)(2,1)}, bf16[2,960,1280]{2,1,0:T(8,128)(2,1)}, u32[]{:S(2)}, u32[]{:S(2)}) collective-permute-start(bf16[2,960,1280]{2,1,0:T(8,128)(2,1)} %bitcast.4.w0_ref), channel_id=1, source_target_pairs={{0,1},{1,0},{2,3},{3,2},{4,5},{5,4},{6,7},{7,6},{8,9},{9,8},{10,11... | collective-permute-start | bytes 14745608 | tf_op jit(solution)/shard_map/ppermute | solution.py:202
  12.4 17.7 %collective-permute-start.4 = (bf16[240,1280]{1,0:T(8,128)(2,1)S(1)}, bf16[240,1280]{1,0:T(8,128)(2,1)S(1)}, u32[]{:S(2)}, u32[]{:S(2)}) collective-permute-start(bf16[240,1280]{1,0:T(8,128)(2,1)S(1)} %get-tuple-element.44), channel_id=1, source_target_pairs={{0,2},{2,0},{1,3},{3,1},{4,6},{6,4},{5,7},{7,5},{8,10},{10,8},{9,1... | collective-permute-start | bytes 1843208 | tf_op jit(solution)/shard_map/ppermute | solution.py:205
  15.4 42.1 %collective-permute-start = (bf16[512,1280]{1,0:T(8,128)(2,1)}, bf16[512,1280]{1,0:T(8,128)(2,1)S(1)}, u32[]{:S(2)}, u32[]{:S(2)}) collective-permute-start(bf16[512,1280]{1,0:T(8,128)(2,1)} %get-tuple-element.84), channel_id=1, source_target_pairs={{0,2},{2,0},{1,3},{3,1},{4,6},{6,4},{5,7},{7,5},{8,10},{10,8},{9,1... | collective-permute-start | bytes 3932168 | tf_op jit(solution)/shard_map/ppermute | solution.py:205
  30.9 212.6 %all-gather.11.cloned.1.call-start = ((), (), s32[]{:S(2)}) async-start(), calls=%async_computation.2 | async-start | bytes 8192000 | tf_op jit(solution)/shard_map/all_gather | solution.py:222
  57.5 37.3 %collective-permute-start.15 = (bf16[2,320,1280]{2,1,0:T(8,128)(2,1)S(1)}, bf16[2,320,1280]{2,1,0:T(8,128)(2,1)}, u32[]{:S(2)}, u32[]{:S(2)}) collective-permute-start(bf16[2,320,1280]{2,1,0:T(8,128)(2,1)S(1)} %pad_maximum_fusion.2), channel_id=1, source_target_pairs={{0,2},{2,0},{1,3},{3,1},{4,6},{6,4},{5,7},{7,5},{8,10},{10,8},{9,1... | collective-permute-start | bytes 4915208 | tf_op jit(solution)/shard_map/ppermute | solution.py:205
  62.5 9.8 %copy-start.3 = (bf16[1024,1280]{1,0:T(8,128)(2,1)}, bf16[1024,1280]{1,0:T(8,128)(2,1)S(1)}, u32[]{:S(2)}) copy-start(bf16[1024,1280]{1,0:T(8,128)(2,1)S(1)} %add_convert_fusion.h_ref) | copy-start | bytes 7864324
  73.6 40.0 %copy-start.19 = (bf16[1024,1024]{1,0:T(8,128)(2,1)}, bf16[1024,1024]{1,0:T(8,128)(2,1)S(1)}, u32[]{:S(2)}) copy-start(bf16[1024,1024]{1,0:T(8,128)(2,1)S(1)} %get-tuple-element.42.q_ref.own_ref) | copy-start | bytes 6291460
  73.6 21.5 %collective-permute-start.2 = (bf16[1024,1024]{1,0:T(8,128)(2,1)S(1)}, bf16[1024,1024]{1,0:T(8,128)(2,1)}, u32[]{:S(2)}, u32[]{:S(2)}) collective-permute-start(bf16[1024,1024]{1,0:T(8,128)(2,1)S(1)} %get-tuple-element.42.q_ref.own_ref), channel_id=1, source_target_pairs={{0,1},{1,0},{2,3},{3,2},{4,5},{5,4},{6,7},{7,6},{8,9},{9,8},{10,11... | collective-permute-start | bytes 6291464 | tf_op jit(solution)/shard_map/ppermute | solution.py:202
  94.8 253.4 %all-gather.9.cloned.1.call-start = ((), (), s32[]{:S(2)}) async-start(), calls=%async_computation.1 | async-start | bytes 3072000 | tf_op jit(solution)/shard_map/all_gather | solution.py:222
  95.1 21.1 %collective-permute-start.3 = (bf16[1024,1024]{1,0:T(8,128)(2,1)}, bf16[1024,1024]{1,0:T(8,128)(2,1)}, u32[]{:S(2)}, u32[]{:S(2)}) collective-permute-start(bf16[1024,1024]{1,0:T(8,128)(2,1)} %copy-done.21), channel_id=1, source_target_pairs={{0,1},{1,0},{2,3},{3,2},{4,5},{5,4},{6,7},{7,6},{8,9},{9,8},{10,11... | collective-permute-start | bytes 6291464 | tf_op jit(solution)/shard_map/ppermute | solution.py:202
  96.8 18.3 %copy-start.39 = (f32[2,1280]{1,0:T(2,128)S(1)}, f32[2,1280]{1,0:T(2,128)}, u32[]{:S(2)}) copy-start(f32[2,1280]{1,0:T(2,128)} %param.13) | copy-start | bytes 30724
  96.8 18.3 %copy-start.41 = (f32[2,1280]{1,0:T(2,128)S(1)}, f32[2,1280]{1,0:T(2,128)}, u32[]{:S(2)}) copy-start(f32[2,1280]{1,0:T(2,128)} %param.15) | copy-start | bytes 30724
  114.6 20.9 %collective-permute-start.5 = (bf16[1,960,1280]{2,1,0:T(8,128)(2,1)}, bf16[1,960,1280]{2,1,0:T(8,128)(2,1)S(1)}, u32[]{:S(2)}, u32[]{:S(2)}) collective-permute-start(bf16[1,960,1280]{2,1,0:T(8,128)(2,1)} %bitcast.35), channel_id=1, source_target_pairs={{0,1},{1,0},{2,3},{3,2},{4,5},{5,4},{6,7},{7,6},{8,9},{9,8},{10,11... | collective-permute-start | bytes 7372808 | tf_op jit(solution)/shard_map/ppermute | solution.py:202
  115.7 104.4 %collective-permute-start.12 = (bf16[2,4,320,1280]{3,2,1,0:T(8,128)(2,1)}, bf16[2,4,320,1280]{3,2,1,0:T(8,128)(2,1)}, u32[]{:S(2)}, u32[]{:S(2)}) collective-permute-start(bf16[2,4,320,1280]{3,2,1,0:T(8,128)(2,1)} %bitcast.42), channel_id=1, source_target_pairs={{0,1},{1,0},{2,3},{3,2},{4,5},{5,4},{6,7},{7,6},{8,9},{9,8},{10,11... | collective-permute-start | bytes 19660808 | tf_op jit(solution)/shard_map/ppermute | solution.py:202
  115.7 19.8 %copy-start.4 = (bf16[1024,1280]{1,0:T(8,128)(2,1)S(1)}, bf16[1024,1280]{1,0:T(8,128)(2,1)}, u32[]{:S(2)}) copy-start(bf16[1024,1280]{1,0:T(8,128)(2,1)} %copy-done.3) | copy-start | bytes 7864324
  115.7 19.8 %copy-start.16 = (bf16[960,1280]{1,0:T(8,128)(2,1)S(1)}, bf16[960,1280]{1,0:T(8,128)(2,1)}, u32[]{:S(2)}) copy-start(bf16[960,1280]{1,0:T(8,128)(2,1)} %all-gather.7.cloned.1.call-done) | copy-start | bytes 7372804
  115.7 104.3 %collective-permute-start.13 = (bf16[2,4,320,1280]{3,2,1,0:T(8,128)(2,1)}, bf16[2,4,320,1280]{3,2,1,0:T(8,128)(2,1)}, u32[]{:S(2)}, u32[]{:S(2)}) collective-permute-start(bf16[2,4,320,1280]{3,2,1,0:T(8,128)(2,1)} %bitcast.46), channel_id=1, source_target_pairs={{0,1},{1,0},{2,3},{3,2},{4,5},{5,4},{6,7},{7,6},{8,9},{9,8},{10,11... | collective-permute-start | bytes 19660808 | tf_op jit(solution)/shard_map/ppermute | solution.py:202
  135.5 6.6 %copy-start.40 = (f32[2,1280]{1,0:T(2,128)S(1)}, f32[2,1280]{1,0:T(2,128)}, u32[]{:S(2)}) copy-start(f32[2,1280]{1,0:T(2,128)} %param.17) | copy-start | bytes 30724
  135.5 7.2 %copy-start = (bf16[2,5,64,1280]{3,2,1,0:T(8,128)(2,1)S(1)}, bf16[2,5,64,1280]{3,2,1,0:T(8,128)(2,1)}, u32[]{:S(2)}) copy-start(bf16[2,5,64,1280]{3,2,1,0:T(8,128)(2,1)} %param.12) | copy-start | bytes 4915204
  142.0 8.7 %collective-permute-start.6 = (bf16[1024,1024]{1,0:T(8,128)(2,1)S(1)}, bf16[1024,1024]{1,0:T(8,128)(2,1)S(1)}, u32[]{:S(2)}, u32[]{:S(2)}) collective-permute-start(bf16[1024,1024]{1,0:T(8,128)(2,1)S(1)} %get-tuple-element.48.q_ref.own_ref), channel_id=1, source_target_pairs={{0,1},{1,0},{2,3},{3,2},{4,5},{5,4},{6,7},{7,6},{8,9},{9,8},{10,11... | collective-permute-start | bytes 6291464 | tf_op jit(solution)/shard_map/ppermute | solution.py:202
  143.7 27.0 %collective-permute-start.7 = (bf16[1024,1024]{1,0:T(8,128)(2,1)}, bf16[1024,1024]{1,0:T(8,128)(2,1)S(1)}, u32[]{:S(2)}, u32[]{:S(2)}) collective-permute-start(bf16[1024,1024]{1,0:T(8,128)(2,1)} %get-tuple-element.46.q_ref.own_ref), channel_id=1, source_target_pairs={{0,1},{1,0},{2,3},{3,2},{4,5},{5,4},{6,7},{7,6},{8,9},{9,8},{10,11... | collective-permute-start | bytes 6291464 | tf_op jit(solution)/shard_map/ppermute | solution.py:202
  145.7 3.5 collective-permute-start.11
  149.2 38.5 %collective-permute-start.14 = (f32[2,1280]{1,0:T(2,128)S(1)}, f32[2,1280]{1,0:T(2,128)S(1)}, u32[]{:S(2)}, u32[]{:S(2)}) collective-permute-start(f32[2,1280]{1,0:T(2,128)S(1)} %copy-done.41), channel_id=1, source_target_pairs={{0,2},{2,0},{1,3},{3,1},{4,6},{6,4},{5,7},{7,5},{8,10},{10,8},{9,1... | collective-permute-start | bytes 30728 | tf_op jit(solution)/shard_map/ppermute | solution.py:205
  150.7 20.6 %copy-start.18 = (bf16[1024,1024]{1,0:T(8,128)(2,1)S(1)}, bf16[1024,1024]{1,0:T(8,128)(2,1)}, u32[]{:S(2)}) copy-start(bf16[1024,1024]{1,0:T(8,128)(2,1)} %copy-done.17) | copy-start | bytes 6291460
  150.7 20.0 %collective-permute-start.9 = (bf16[1,320,1280]{2,1,0:T(8,128)(2,1)S(1)}, bf16[1,320,1280]{2,1,0:T(8,128)(2,1)}, u32[]{:S(2)}, u32[]{:S(2)}) collective-permute-start(bf16[1,320,1280]{2,1,0:T(8,128)(2,1)S(1)} %bitcast.54), channel_id=1, source_target_pairs={{0,2},{2,0},{1,3},{3,1},{4,6},{6,4},{5,7},{7,5},{8,10},{10,8},{9,1... | collective-permute-start | bytes 2457608 | tf_op jit(solution)/shard_map/ppermute | solution.py:205
  169.8 17.9 %copy-start.37 = (bf16[240,1280]{1,0:T(8,128)(2,1)S(1)}, bf16[240,1280]{1,0:T(8,128)(2,1)}, u32[]{:S(2)}) copy-start(bf16[240,1280]{1,0:T(8,128)(2,1)} %get-tuple-element.63) | copy-start | bytes 1843204
  170.7 32.8 %collective-permute-start.8 = (bf16[2,320,1280]{2,1,0:T(8,128)(2,1)S(1)}, bf16[2,320,1280]{2,1,0:T(8,128)(2,1)S(1)}, u32[]{:S(2)}, u32[]{:S(2)}) collective-permute-start(bf16[2,320,1280]{2,1,0:T(8,128)(2,1)S(1)} %bitcast.30), channel_id=1, source_target_pairs={{0,1},{1,0},{2,3},{3,2},{4,5},{5,4},{6,7},{7,6},{8,9},{9,8},{10,11... | collective-permute-start | bytes 4915208 | tf_op jit(solution)/shard_map/ppermute | solution.py:202
  170.7 32.8 %collective-permute-start.10 = (bf16[1,320,1280]{2,1,0:T(8,128)(2,1)}, bf16[1,320,1280]{2,1,0:T(8,128)(2,1)}, u32[]{:S(2)}, u32[]{:S(2)}) collective-permute-start(bf16[1,320,1280]{2,1,0:T(8,128)(2,1)} %collective-permute-done.9.w2), channel_id=1, source_target_pairs={{0,1},{1,0},{2,3},{3,2},{4,5},{5,4},{6,7},{7,6},{8,9},{9,8},{10,11... | collective-permute-start | bytes 2457608 | tf_op jit(solution)/shard_map/ppermute | solution.py:202
  187.7 15.8 %collective-permute-start.20 = (bf16[240,1280]{1,0:T(8,128)(2,1)S(1)}, bf16[240,1280]{1,0:T(8,128)(2,1)}, u32[]{:S(2)}, u32[]{:S(2)}) collective-permute-start(bf16[240,1280]{1,0:T(8,128)(2,1)S(1)} %copy-done.37), channel_id=1, source_target_pairs={{0,2},{2,0},{1,3},{3,1},{4,6},{6,4},{5,7},{7,5},{8,10},{10,8},{9,1... | collective-permute-start | bytes 1843208 | tf_op jit(solution)/shard_map/ppermute | solution.py:205
  203.5 162.3 %all-gather.13.cloned.1.call-start = ((), (), s32[]{:S(2)}) async-start(), calls=%async_computation.3 | async-start | bytes 8192000 | tf_op jit(solution)/shard_map/all_gather | solution.py:222
  243.5 55.4 %collective-permute-start.17 = (bf16[4,2,320,1280]{3,2,1,0:T(8,128)(2,1)}, bf16[4,2,320,1280]{3,2,1,0:T(8,128)(2,1)}, u32[]{:S(2)}, u32[]{:S(2)}) collective-permute-start(bf16[4,2,320,1280]{3,2,1,0:T(8,128)(2,1)} %bitcast.50), channel_id=1, source_target_pairs={{0,1},{1,0},{2,3},{3,2},{4,5},{5,4},{6,7},{7,6},{8,9},{9,8},{10,11... | collective-permute-start | bytes 19660808 | tf_op jit(solution)/shard_map/ppermute | solution.py:202
  258.9 38.2 %collective-permute-start.26 = (bf16[2,320,1280]{2,1,0:T(8,128)(2,1)}, bf16[2,320,1280]{2,1,0:T(8,128)(2,1)}, u32[]{:S(2)}, u32[]{:S(2)}) collective-permute-start(bf16[2,320,1280]{2,1,0:T(8,128)(2,1)} %pad_maximum_fusion.3), channel_id=1, source_target_pairs={{0,2},{2,0},{1,3},{3,1},{4,6},{6,4},{5,7},{7,5},{8,10},{10,8},{9,1... | collective-permute-start | bytes 4915208 | tf_op jit(solution)/shard_map/ppermute | solution.py:205
  297.1 1.2 collective-permute-start.16
  325.7 4.2 collective-permute-start.18
  327.2 38.6 %collective-permute-start.19 = (bf16[1024,1024]{1,0:T(8,128)(2,1)}, bf16[1024,1024]{1,0:T(8,128)(2,1)}, u32[]{:S(2)}, u32[]{:S(2)}) collective-permute-start(bf16[1024,1024]{1,0:T(8,128)(2,1)} %get-tuple-element.59.q_ref.own_ref), channel_id=1, source_target_pairs={{0,1},{1,0},{2,3},{3,2},{4,5},{5,4},{6,7},{7,6},{8,9},{9,8},{10,11... | collective-permute-start | bytes 6291464 | tf_op jit(solution)/shard_map/ppermute | solution.py:202
  348.2 36.4 %collective-permute-start.21 = (bf16[1,960,1280]{2,1,0:T(8,128)(2,1)}, bf16[1,960,1280]{2,1,0:T(8,128)(2,1)}, u32[]{:S(2)}, u32[]{:S(2)}) collective-permute-start(bf16[1,960,1280]{2,1,0:T(8,128)(2,1)} %bitcast.33), channel_id=1, source_target_pairs={{0,1},{1,0},{2,3},{3,2},{4,5},{5,4},{6,7},{7,6},{8,9},{9,8},{10,11... | collective-permute-start | bytes 7372808 | tf_op jit(solution)/shard_map/ppermute | solution.py:202
  365.8 18.8 %copy-start.15 = (bf16[960,1280]{1,0:T(8,128)(2,1)S(1)}, bf16[960,1280]{1,0:T(8,128)(2,1)}, u32[]{:S(2)}) copy-start(bf16[960,1280]{1,0:T(8,128)(2,1)} %all-gather.9.cloned.1.call-done) | copy-start | bytes 7372804
  365.8 99.2 %collective-permute-start.27 = (bf16[4,2,320,1280]{3,2,1,0:T(8,128)(2,1)}, bf16[4,2,320,1280]{3,2,1,0:T(8,128)(2,1)}, u32[]{:S(2)}, u32[]{:S(2)}) collective-permute-start(bf16[4,2,320,1280]{3,2,1,0:T(8,128)(2,1)} %bitcast.37), channel_id=1, source_target_pairs={{0,1},{1,0},{2,3},{3,2},{4,5},{5,4},{6,7},{7,6},{8,9},{9,8},{10,11... | collective-permute-start | bytes 19660808 | tf_op jit(solution)/shard_map/ppermute | solution.py:202
  386.4 8.7 %copy-start.35 = (bf16[1,5,64,1280]{3,2,1,0:T(8,128)(2,1)S(1)}, bf16[1,5,64,1280]{3,2,1,0:T(8,128)(2,1)}, u32[]{:S(2)}) copy-start(bf16[1,5,64,1280]{3,2,1,0:T(8,128)(2,1)} %get-tuple-element.85) | copy-start | bytes 2457604
  394.6 21.0 %collective-permute-start.22 = (bf16[1024,1024]{1,0:T(8,128)(2,1)S(1)}, bf16[1024,1024]{1,0:T(8,128)(2,1)S(1)}, u32[]{:S(2)}, u32[]{:S(2)}) collective-permute-start(bf16[1024,1024]{1,0:T(8,128)(2,1)S(1)} %get-tuple-element.67.q_ref.own_ref), channel_id=1, source_target_pairs={{0,1},{1,0},{2,3},{3,2},{4,5},{5,4},{6,7},{7,6},{8,9},{9,8},{10,11... | collective-permute-start | bytes 6291464 | tf_op jit(solution)/shard_map/ppermute | solution.py:202
  395.0 41.4 %collective-permute-start.23 = (bf16[1024,1024]{1,0:T(8,128)(2,1)}, bf16[1024,1024]{1,0:T(8,128)(2,1)}, u32[]{:S(2)}, u32[]{:S(2)}) collective-permute-start(bf16[1024,1024]{1,0:T(8,128)(2,1)} %get-tuple-element.65.q_ref.own_ref), channel_id=1, source_target_pairs={{0,1},{1,0},{2,3},{3,2},{4,5},{5,4},{6,7},{7,6},{8,9},{9,8},{10,11... | collective-permute-start | bytes 6291464 | tf_op jit(solution)/shard_map/ppermute | solution.py:202
  395.1 20.5 %collective-permute-start.24 = (bf16[1,320,1280]{2,1,0:T(8,128)(2,1)S(1)}, bf16[1,320,1280]{2,1,0:T(8,128)(2,1)S(1)}, u32[]{:S(2)}, u32[]{:S(2)}) collective-permute-start(bf16[1,320,1280]{2,1,0:T(8,128)(2,1)S(1)} %bitcast.53), channel_id=1, source_target_pairs={{0,2},{2,0},{1,3},{3,1},{4,6},{6,4},{5,7},{7,5},{8,10},{10,8},{9,1... | collective-permute-start | bytes 2457608 | tf_op jit(solution)/shard_map/ppermute | solution.py:205
  415.6 37.9 %collective-permute-start.25 = (bf16[1,320,1280]{2,1,0:T(8,128)(2,1)S(1)}, bf16[1,320,1280]{2,1,0:T(8,128)(2,1)S(1)}, u32[]{:S(2)}, u32[]{:S(2)}) collective-permute-start(bf16[1,320,1280]{2,1,0:T(8,128)(2,1)S(1)} %collective-permute-done.24.w2), channel_id=1, source_target_pairs={{0,1},{1,0},{2,3},{3,2},{4,5},{5,4},{6,7},{7,6},{8,9},{9,8},{10,11... | collective-permute-start | bytes 2457608 | tf_op jit(solution)/shard_map/ppermute | solution.py:202
  436.4 17.1 %copy-start.10 = (bf16[1024,320]{1,0:T(8,128)(2,1)S(1)}, bf16[1024,320]{1,0:T(8,128)(2,1)}, u32[]{:S(2)}) copy-start(bf16[1024,320]{1,0:T(8,128)(2,1)} %copy-done.9) | copy-start | bytes 1966084
  486.5 31.2 %collective-permute-start.28 = (bf16[512,1280]{1,0:T(8,128)(2,1)}, bf16[512,1280]{1,0:T(8,128)(2,1)S(1)}, u32[]{:S(2)}, u32[]{:S(2)}) collective-permute-start(bf16[512,1280]{1,0:T(8,128)(2,1)} %shard_map.108), channel_id=1, source_target_pairs={{0,2},{2,0},{1,3},{3,1},{4,6},{6,4},{5,7},{7,5},{8,10},{10,8},{9,1... | collective-permute-start | bytes 3932168 | tf_op jit(solution)/shard_map/ppermute | solution.py:205
  (27 other events, 50.2 us)
Sparse Core Ops, SparseCore 0:
  31.0 35.7 all-gather.6
  94.9 69.3 all-gather.10
  203.6 34.3 all-gather.8
  297.2 68.5 all-gather.12
